TPU v7x, 256 devices: a whole 4x4x8 slice. The times are simulated.
256 devices in a mesh: slab: 64 (over z, y, core), pencil: 4 (over x).
Axes of the slice: x: 4, y: 4, z: 8, core: 2. Of those that a mesh axis runs over, the one named last changes fastest.
Arguments:
- density_history: float32 [7, 512, 320, 320], P(None, 'slab', 'pencil'), may hold values from -6 to 6
- residual_history: float32 [7, 512, 320, 320], P(None, 'slab', 'pencil'), as said below
- occupancy_history: float32 [7, 6144, 324], P(None, ('slab', 'pencil')), may hold values from -6 to 6
- occupancy_residual: float32 [7, 6144, 324], P(None, ('slab', 'pencil')), may hold values from -6 to 6
- species: int32 [6144], P(('slab', 'pencil')), may hold values from 0 to 3
- slot_count: int32 [256], P(('slab', 'pencil')), may hold values from 12 to 24, as said below
Outputs:
- new_density: float32 [512, 320, 320], P('slab', 'pencil')
- new_occupancy: float32 [6144, 324], P(('slab', 'pencil'))
Inputs may be any that keep to these rules, and one draw needn't show every extreme that they name: `residual_history`: residual fields of the 7 previous steps. Device d of slab+pencil (slab slowest) holds slots d * 24 to (d + 1) * 24 - 1, of which the first slot_count[d] hold atoms; some device is full in every draw.
All inputs are finite; a program needn't handle non-finite values.
Results may differ from a plain program's by a relative error of at most 0.00017.
Values sent between devices are 32-bit elements; how exact they have to be, the bound alone decides.
No kernel may reach another device: no remote copies, remote signals or barrier semaphores. Data moves between devices by JAX's collectives and lax.ppermute only.
A program may use at most 128 MiB of HBM per device.

v0:
```python
import functools
import math

import jax
import jax.numpy as jnp
import numpy as np
from jax import lax
from jax.experimental import pallas as pl
from jax.experimental.pallas import tpu as pltpu
from jax.sharding import Mesh
from jax.sharding import PartitionSpec as P

ORBITALS = 18
SLAB = ("slab_0", "slab_1", "slab_2")
SLAB_PENCIL = ("slab_0", "slab_1", "slab_2", "pencil")

grid_mixing = 0.5
block_mixing = 0.5
kerker_wave = 6.0
species_orbitals = (18, 13, 8, 5)

f32 = jnp.float32
bf16 = jnp.bfloat16
LANES = 128
MIB = 1 << 20


def pair_list(histories):
    return [(i, j) for i in range(histories) for j in range(i, histories)]


def split(value):
    high = value.astype(bf16)
    return high, (value - high.astype(f32)).astype(bf16)


def product(left, right, dims):
    dot = functools.partial(
        lax.dot_general, dimension_numbers=(dims, ((), ())), preferred_element_type=f32
    )
    return dot(left[0], right[0]) + (dot(left[0], right[1]) + dot(left[1], right[0]))


def hartley(rows, columns, length):
    angle = (np.outer(rows, columns) % length) * (2.0 * math.pi / length)
    table = np.cos(angle) + np.sin(angle)
    high = table.astype(bf16)
    low = (table - high.astype(np.float64)).astype(bf16)
    return high, low


def block_mask(species_ref, count_ref, slots, entries):
    row = lax.broadcasted_iota(jnp.int32, (slots, entries), 0)
    entry = lax.broadcasted_iota(jnp.int32, (slots, entries), 1)
    row_index = (entry * 3641) >> 16
    column_index = entry - ORBITALS * row_index
    limit = jnp.zeros((slots, entries), jnp.int32)
    for slot in range(slots):
        kind = species_ref[slot]
        number = jnp.int32(0)
        for index, orbital_number in enumerate(species_orbitals):
            number = jnp.where(kind == index, jnp.int32(orbital_number), number)
        number = jnp.where(slot < count_ref[0], number, jnp.int32(0))
        limit = jnp.where(row == slot, number, limit)
    return (row_index < limit) & (column_index < limit)


def gram_kernel(
    species_ref, count_ref, residual_ref, block_ref, out_ref, acc_ref, *, cell_total, block_total
):
    step = pl.program_id(0)
    histories, _, rows, width = residual_ref.shape
    pairs = pair_list(histories)

    @pl.when(step == 0)
    def _():
        acc_ref[...] = jnp.zeros_like(acc_ref)

    for start in range(0, width, LANES):
        lanes = slice(start, min(start + LANES, width))
        accs = [acc_ref[k, :, lanes] for k in range(len(pairs))]
        for top in range(0, rows, 8):
            values = [residual_ref[i, 0, top : top + 8, lanes] for i in range(histories)]
            accs = [acc + values[i] * values[j] for acc, (i, j) in zip(accs, pairs)]
        for k, acc in enumerate(accs):
            acc_ref[k, :, lanes] = acc

    @pl.when(step == pl.num_programs(0) - 1)
    def _():
        _, slots, entries = block_ref.shape
        mask = block_mask(species_ref, count_ref, slots, entries)
        blocks = [jnp.where(mask, block_ref[i], 0.0) for i in range(histories)]
        lane = lax.broadcasted_iota(jnp.int32, (1, LANES), 1)
        line = jnp.zeros((1, LANES), f32)
        for k, (i, j) in enumerate(pairs):
            grid_part = jnp.sum(acc_ref[k], axis=(0, 1), keepdims=True) / cell_total
            block_part = jnp.sum(blocks[i] * blocks[j], axis=(0, 1), keepdims=True) / block_total
            line = jnp.where(lane == k, grid_part + block_part, line)
        out_ref[...] = jnp.broadcast_to(line, out_ref.shape)


def mixing_weights(line, histories):
    lane = lax.broadcasted_iota(jnp.int32, (1, LANES), 1)
    entry = {}
    for k, (i, j) in enumerate(pair_list(histories)):
        entry[j, i] = jnp.sum(jnp.where(lane == k, line, 0.0), axis=1, keepdims=True)
    factor = {}
    inverse = {}
    work = dict(entry)
    for k in range(histories):
        inverse[k] = 1.0 / work[k, k]
        for i in range(k + 1, histories):
            factor[i, k] = work[i, k] * inverse[k]
        for i in range(k + 1, histories):
            for j in range(k + 1, i + 1):
                work[i, j] = work[i, j] - factor[i, k] * work[j, k]
    solved = [jnp.ones((1, 1), f32) for _ in range(histories)]
    for i in range(histories):
        for k in range(i):
            solved[i] = solved[i] - factor[i, k] * solved[k]
    solved = [value * inverse[i] for i, value in enumerate(solved)]
    for i in reversed(range(histories)):
        for k in range(i + 1, histories):
            solved[i] = solved[i] - factor[k, i] * solved[k]
    total = solved[0]
    for value in solved[1:]:
        total = total + value
    return [value / total for value in solved]


def mix_kernel(
    sums_ref, residual_ref, high_ref, low_ref, out_ref, weights_ref, mixed_high, mixed_low
):
    step = pl.program_id(0)
    histories, _, rows, width = residual_ref.shape

    @pl.when(step == 0)
    def _():
        line = jnp.sum(sums_ref[...], axis=0, keepdims=True)
        weights = mixing_weights(line, histories)
        for i, weight in enumerate(weights):
            weights_ref[i : i + 1, :] = jnp.broadcast_to(weight, (1, LANES))
        weights_ref[histories:, :] = jnp.zeros((8 - histories, LANES), f32)

    weights = [weights_ref[i : i + 1, 0:1] for i in range(histories)]
    mixed = weights[0] * residual_ref[0, 0]
    for i in range(1, histories):
        mixed = mixed + weights[i] * residual_ref[i, 0]
    high, low = split(mixed)
    mixed_high[pl.ds(step * rows, rows), :] = high
    mixed_low[pl.ds(step * rows, rows), :] = low

    @pl.when(step == pl.num_programs(0) - 1)
    def _():
        table = (high_ref[...], low_ref[...])
        result = product(table, (mixed_high[...], mixed_low[...]), ((1,), (1,)))
        pieces = result.shape[1] // LANES
        for piece in range(pieces):
            out_ref[pl.ds(piece, result.shape[0], stride=pieces), :] = result[
                :, piece * LANES : (piece + 1) * LANES
            ]


def z_forward_kernel(in_ref, high_ref, low_ref, out_ref, lines_ref, *, slab_count, z_local, y_local):
    z_length = slab_count * z_local
    per_slab = in_ref.shape[0] // slab_count
    pieces = z_local * y_local // LANES
    columns = per_slab // pieces
    for column in range(columns):
        turned = []
        for piece in range(pieces):
            block = in_ref[pl.ds(column * pieces + piece, slab_count, stride=per_slab), :]
            turned.append(block.T)
        turned = jnp.concatenate(turned, axis=0)
        lines_ref[column * y_local : (column + 1) * y_local, :] = jnp.concatenate(
            [turned[z * y_local : (z + 1) * y_local, :] for z in range(z_local)], axis=1
        )
    result = product(split(lines_ref[...]), (high_ref[...], low_ref[...]), ((1,), (0,)))
    for part in range(z_length // LANES):
        out_ref[part] = result[:, part * LANES : (part + 1) * LANES]


def filter_kernel(
    place_ref, in_ref, high_ref, low_ref, out_ref, *, kx_local, x_length, y_length, z_length, scale
):
    pencil_count, _, kz_local = in_ref.shape
    y_local = y_length // pencil_count
    table = (high_ref[...], low_ref[...])
    lines = jnp.concatenate(
        [
            jnp.concatenate(
                [in_ref[q, j * y_local : (j + 1) * y_local, :] for q in range(pencil_count)], axis=0
            )
            for j in range(kx_local)
        ],
        axis=1,
    )
    spectrum = product(table, split(lines), ((1,), (0,)))
    freq_y = lax.broadcasted_iota(jnp.int32, (y_length, kz_local), 0)
    freq_z = lax.broadcasted_iota(jnp.int32, (y_length, kz_local), 1) + place_ref[1] * kz_local
    mag_y = jnp.minimum(freq_y, y_length - freq_y).astype(f32)
    mag_z = jnp.minimum(freq_z, z_length - freq_z).astype(f32)
    plane = mag_y * mag_y + mag_z * mag_z
    kept = []
    for j in range(kx_local):
        freq_x = place_ref[0] * kx_local + j
        mag_x = jnp.minimum(freq_x, x_length - freq_x).astype(f32)
        square = plane + mag_x * mag_x
        factor = square / (square + kerker_wave * kerker_wave) * scale
        kept.append(spectrum[:, j * kz_local : (j + 1) * kz_local] * factor)
    result = product(table, split(jnp.concatenate(kept, axis=1)), ((1,), (0,)))
    for q in range(pencil_count):
        for j in range(kx_local):
            out_ref[q, j * y_local : (j + 1) * y_local, :] = result[
                q * y_local : (q + 1) * y_local, j * kz_local : (j + 1) * kz_local
            ]


def z_inverse_kernel(in_ref, high_ref, low_ref, out_ref, *, slab_count, z_local, y_local):
    parts = in_ref.shape[0]
    per_slab = out_ref.shape[0] // slab_count
    pieces = z_local * y_local // LANES
    columns = per_slab // pieces
    lines = jnp.concatenate([in_ref[part] for part in range(parts)], axis=1)
    result = product(split(lines), (high_ref[...], low_ref[...]), ((1,), (1,)))
    for column in range(columns):
        block = result[column * y_local : (column + 1) * y_local, :]
        stacked = jnp.concatenate(
            [block[:, z * slab_count : (z + 1) * slab_count] for z in range(z_local)], axis=0
        )
        for piece in range(pieces):
            out_ref[pl.ds(column * pieces + piece, slab_count, stride=per_slab), :] = stacked[
                piece * LANES : (piece + 1) * LANES, :
            ].T


def mean_kernel(
    species_ref, count_ref, weights_ref, density_ref, block_ref, block_residual_ref, out_ref, out_block_ref
):
    step = pl.program_id(0)
    histories = density_ref.shape[0]
    weights = [weights_ref[i : i + 1, 0:1] for i in range(histories)]
    mean = weights[0] * density_ref[0, 0]
    for i in range(1, histories):
        mean = mean + weights[i] * density_ref[i, 0]
    out_ref[0] = mean

    @pl.when(step == 0)
    def _():
        _, slots, entries = block_ref.shape
        mask = block_mask(species_ref, count_ref, slots, entries)
        total = weights[0] * (block_ref[0] + block_mixing * block_residual_ref[0])
        for i in range(1, histories):
            total = total + weights[i] * (block_ref[i] + block_mixing * block_residual_ref[i])
        out_block_ref[...] = jnp.where(mask, total, 0.0)


def x_inverse_kernel(in_ref, mean_ref, high_ref, low_ref, out_ref):
    z_local, y_local, x_length = mean_ref.shape
    table = (high_ref[...], low_ref[...])
    pieces = z_local * y_local // LANES
    fields = []
    for piece in range(pieces):
        block = in_ref[pl.ds(piece, x_length, stride=pieces), :]
        fields.append(product(split(block.T), table, ((1,), (0,))))
    field = jnp.concatenate(fields, axis=0)
    for z in range(z_local):
        out_ref[z] = mean_ref[z] + field[z * y_local : (z + 1) * y_local, :]


def whole():
    return pl.BlockSpec(memory_space=pltpu.VMEM)


def scalars():
    return pl.BlockSpec(memory_space=pltpu.SMEM)


def params(limit):
    return pltpu.CompilerParams(vmem_limit_bytes=limit * MIB)


def body(
    density_history, residual_history, occupancy_history, occupancy_residual, species, slot_count
):
    histories, z_local, y_local, x_length = residual_history.shape
    slab_count = lax.axis_size(SLAB)
    pencil_count = lax.axis_size("pencil")
    devices = slab_count * pencil_count
    y_length = y_local * pencil_count
    z_length = z_local * slab_count
    slots, entries = occupancy_residual.shape[1:]
    kx_local = x_length // slab_count
    kz_local = z_length // pencil_count
    lines = kx_local * y_local
    rows = z_local * y_local * x_length // LANES
    cell_total = float(z_length * y_length * x_length)
    x_table = hartley(np.arange(x_length), np.arange(x_length), x_length)
    y_table = hartley(np.arange(y_length), np.arange(y_length), y_length)
    z_order = (np.arange(slab_count)[None, :] * z_local + np.arange(z_local)[:, None]).reshape(-1)
    z_table = hartley(z_order, np.arange(z_length), z_length)

    plane_in = pl.BlockSpec((histories, 1, y_local, x_length), lambda z: (0, z, 0, 0))
    sums = pl.pallas_call(
        functools.partial(
            gram_kernel, cell_total=cell_total, block_total=100.0 * slots * devices
        ),
        grid=(z_local,),
        in_specs=[scalars(), scalars(), plane_in, whole()],
        out_specs=whole(),
        out_shape=jax.ShapeDtypeStruct((devices, LANES), f32),
        scratch_shapes=[pltpu.VMEM((len(pair_list(histories)), 8, x_length), f32)],
        compiler_params=params(16),
        name="gram",
    )(species, slot_count, residual_history, occupancy_residual)
    sums = lax.all_to_all(
        sums.reshape(devices, 1, LANES), SLAB_PENCIL, split_axis=0, concat_axis=0, tiled=True
    ).reshape(devices, LANES)

    packed, weights = pl.pallas_call(
        mix_kernel,
        grid=(z_local,),
        in_specs=[whole(), plane_in, whole(), whole()],
        out_specs=[whole(), whole()],
        out_shape=[
            jax.ShapeDtypeStruct((rows, LANES), f32),
            jax.ShapeDtypeStruct((8, LANES), f32),
        ],
        scratch_shapes=[
            pltpu.VMEM((z_local * y_local, x_length), bf16),
            pltpu.VMEM((z_local * y_local, x_length), bf16),
        ],
        compiler_params=params(24),
        name="mix",
    )(sums, residual_history, *x_table)

    def slab_move(array):
        shape = (slab_count, rows // slab_count, 1, LANES)
        return lax.all_to_all(
            array.reshape(shape), SLAB, split_axis=0, concat_axis=0, tiled=True
        ).reshape(rows, LANES)

    def pencil_move(array):
        return lax.all_to_all(array, "pencil", split_axis=0, concat_axis=0, tiled=True)

    sizes = dict(slab_count=slab_count, z_local=z_local, y_local=y_local)
    moved = slab_move(packed)
    mean, new_occupancy = pl.pallas_call(
        mean_kernel,
        grid=(z_local,),
        in_specs=[scalars(), scalars(), whole(), plane_in, whole(), whole()],
        out_specs=[pl.BlockSpec((1, y_local, x_length), lambda z: (z, 0, 0)), whole()],
        out_shape=[
            jax.ShapeDtypeStruct((z_local, y_local, x_length), f32),
            jax.ShapeDtypeStruct((slots, entries), f32),
        ],
        compiler_params=params(16),
        name="mean",
    )(species, slot_count, weights, density_history, occupancy_history, occupancy_residual)
    spectrum = pl.pallas_call(
        functools.partial(z_forward_kernel, **sizes),
        in_specs=[whole()] * 3,
        out_specs=whole(),
        out_shape=jax.ShapeDtypeStruct((pencil_count, lines, kz_local), f32),
        scratch_shapes=[pltpu.VMEM((lines, z_length), f32)],
        compiler_params=params(24),
        name="z_forward",
    )(moved, *z_table)
    moved = pencil_move(spectrum)
    place = jnp.stack([lax.axis_index(SLAB), lax.axis_index("pencil")]).astype(jnp.int32)
    kept = pl.pallas_call(
        functools.partial(
            filter_kernel,
            kx_local=kx_local,
            x_length=x_length,
            y_length=y_length,
            z_length=z_length,
            scale=grid_mixing / cell_total,
        ),
        in_specs=[scalars(), whole(), whole(), whole()],
        out_specs=whole(),
        out_shape=jax.ShapeDtypeStruct((pencil_count, lines, kz_local), f32),
        compiler_params=params(24),
        name="filter",
    )(place, moved, *y_table)
    moved = pencil_move(kept)
    packed = pl.pallas_call(
        functools.partial(z_inverse_kernel, **sizes),
        in_specs=[whole()] * 3,
        out_specs=whole(),
        out_shape=jax.ShapeDtypeStruct((rows, LANES), f32),
        compiler_params=params(24),
        name="z_inverse",
    )(moved, *z_table)
    moved = slab_move(packed)
    new_density = pl.pallas_call(
        x_inverse_kernel,
        in_specs=[whole()] * 4,
        out_specs=whole(),
        out_shape=jax.ShapeDtypeStruct((z_local, y_local, x_length), f32),
        compiler_params=params(24),
        name="x_inverse",
    )(moved, mean, *x_table)
    return (new_density, new_occupancy)


def solution(mesh):
    torus = Mesh(
        mesh.devices.reshape(8, 4, 2, mesh.shape["pencil"]),
        ("slab_0", "slab_1", "slab_2", "pencil"),
    )
    placed = (
        P(None, SLAB, "pencil", None),
        P(None, SLAB, "pencil", None),
        P(None, SLAB_PENCIL, None),
        P(None, SLAB_PENCIL, None),
        P(SLAB_PENCIL),
        P(SLAB_PENCIL),
    )
    return jax.shard_map(
        body,
        mesh=torus,
        in_specs=placed,
        out_specs=(P(SLAB, "pencil", None), P(SLAB_PENCIL, None)),
        check_vma=False,
    )
```

profile of v0, /device:TPU:1, one launch (start us, length us, event | category | flops | bytes accessed | tf_op | source)
XLA Modules:
  0.0 138.0 jit_solution(9143186634754669776)
XLA Ops:
  1.3 0.0 copy-start
  1.3 2.9 %copy-done = f32[7,8,80,320]{3,2,1,0:T(8,128)S(1)} copy-done((f32[7,8,80,320]{3,2,1,0:T(8,128)S(1)}, f32[7,8,80,320]{3,2,1,0:T(8,128)}, u32[]{:S(2)}) %copy-start) | copy-done | bytes 5734424
  4.2 0.0 copy-start.7
  4.2 0.9 copy-done.7
  5.2 0.0 copy-start.10
  5.2 0.7 copy-done.10
  5.8 0.0 copy-start.1
  5.8 0.0 copy-start.3
  5.8 0.0 copy-start.4
  5.8 0.0 copy-start.5
  5.8 0.0 copy-start.6
  5.9 3.4 %gram.1 = f32[256,128]{1,0:T(8,128)S(1)} custom-call(s32[24]{0:T(128)S(1)} %copy-done.10, s32[1]{0:T(128)S(6)} %copy.17.count_ref, f32[7,8,80,320]{3,2,1,0:T(8,128)S(1)} %copy-done, f32[7,24,324]{2,1,0:T(8,128)S(1)} %copy-done.7), custom_call_target="tpu_custom_call" | custom-call | tf_op jit(solution)/shard_map/gram/pallas_call | solution.py:304
  9.2 28.2 %all_to_all.25 = f32[256,1,128]{2,1,0:T(1,128)S(1)} all-to-all(f32[256,1,128]{2,1,0:T(1,128)S(1)} %bitcast.14), channel_id=1, replica_groups=mesh['slab_0'=8,'slab_1'=4,'slab_2'=2,'pencil'=4] {'slab_0','slab_1','sl..., dimensions={0} | all-to-all | bytes 262144 | tf_op jit(solution)/shard_map/all_to_all | solution.py:316
  37.5 0.0 copy-done.1
  37.5 0.0 copy-done.3
  37.5 0.0 copy-done.4
  37.5 2.7 %mix.1 = (f32[1600,128]{1,0:T(8,128)S(1)}, f32[8,128]{1,0:T(8,128)S(1)}) custom-call(f32[256,128]{1,0:T(8,128)S(1)} %bitcast.13, f32[7,8,80,320]{3,2,1,0:T(8,128)S(1)} %copy-done.1, bf16[320,320]{1,0:T(8,128)(2,1)S(1)} %copy-done.4, bf16[320,320]{1,0:T(8,128)(2,1)S(1)} %copy-done.3), custom_call_target="tpu_custom_call" | custom-call | tf_op jit(solution)/shard_map/mix/pallas_call | solution.py:320
  40.2 0.0 copy-start.8
  40.2 0.0 copy-start.9
  40.3 0.0 copy-start.11
  40.3 28.2 %all_to_all.26 = f32[64,25,1,128]{3,2,1,0:T(1,128)S(1)} all-to-all(f32[64,25,1,128]{3,2,1,0:T(1,128)S(1)} %bitcast.12), channel_id=1, replica_groups=mesh['slab_0'=8,'slab_1'=4,'slab_2'=2,'pencil'=4] {'slab_0','slab_1','sl..., dimensions={0} | all-to-all | bytes 1638400 | tf_op jit(solution)/shard_map/all_to_all | solution.py:339
  68.5 0.0 copy-done.5
  68.5 0.0 copy-done.6
  68.5 2.2 %z_forward.1 = f32[4,400,128]{2,1,0:T(8,128)} custom-call(f32[1600,128]{1,0:T(8,128)S(1)} %bitcast.11, bf16[512,512]{1,0:T(8,128)(2,1)S(1)} %copy-done.6, bf16[512,512]{1,0:T(8,128)(2,1)S(1)} %copy-done.5), custom_call_target="tpu_custom_call" | custom-call | tf_op jit(solution)/shard_map/z_forward/pallas_call | solution.py:360
  70.7 3.5 %all-to-all-start.2 = ((f32[4,400,128]{2,1,0:T(8,128)}), f32[4,400,128]{2,1,0:T(8,128)S(1)}, u32[]{:S(2)}, u32[]{:S(2)}) async-start(f32[4,400,128]{2,1,0:T(8,128)} %z_forward.1), calls=%async_computation.2 | async-start | bytes 1638400 | tf_op jit(solution)/shard_map/all_to_all | solution.py:344
  74.2 0.1 pad_add_fusion.place_ref
  74.3 11.9 %all-to-all-done.2.in_ref = f32[4,400,128]{2,1,0:T(8,128)S(1)} async-done(((f32[4,400,128]{2,1,0:T(8,128)}), f32[4,400,128]{2,1,0:T(8,128)S(1)}, u32[]{:S(2)}, u32[]{:S(2)}) %all-to-all-start.2) | async-done | bytes 819232 | tf_op jit(solution)/shard_map/all_to_all | solution.py:344
  86.2 2.2 %filter.1 = f32[4,400,128]{2,1,0:T(8,128)S(1)} custom-call(s32[2]{0:T(128)S(1)} %pad_add_fusion.place_ref, f32[4,400,128]{2,1,0:T(8,128)S(1)} %all-to-all-done.2.in_ref, bf16[320,320]{1,0:T(8,128)(2,1)S(1)} %copy-done.4, bf16[320,320]{1,0:T(8,128)(2,1)S(1)} %copy-done.3), custom_call_target="tpu_custom_call" | custom-call | tf_op jit(solution)/shard_map/filter/pallas_call | solution.py:371
  88.4 13.2 %all_to_all.27.in_ref = f32[4,400,128]{2,1,0:T(8,128)S(1)} all-to-all(f32[4,400,128]{2,1,0:T(8,128)S(1)} %filter.1), channel_id=1, replica_groups=mesh['slab_0'=8,'slab_1'=4,'slab_2'=2,'pencil'=4] {'pencil'}, dimensions={0} | all-to-all | bytes 1638400 | tf_op jit(solution)/shard_map/all_to_all | solution.py:344
  101.6 2.4 %z_inverse.1 = f32[1600,128]{1,0:T(8,128)} custom-call(f32[4,400,128]{2,1,0:T(8,128)S(1)} %all_to_all.27.in_ref, bf16[512,512]{1,0:T(8,128)(2,1)S(1)} %copy-done.6, bf16[512,512]{1,0:T(8,128)(2,1)S(1)} %copy-done.5), custom_call_target="tpu_custom_call" | custom-call | tf_op jit(solution)/shard_map/z_inverse/pallas_call | solution.py:387
  104.0 8.1 %all-to-all-start.4 = ((f32[64,25,1,128]{3,2,1,0:T(1,128)}), f32[64,25,1,128]{3,2,1,0:T(1,128)S(1)}, u32[]{:S(2)}, u32[]{:S(2)}) async-start(f32[64,25,1,128]{3,2,1,0:T(1,128)} %bitcast.7), calls=%async_computation.4 | async-start | bytes 1638400 | tf_op jit(solution)/shard_map/all_to_all | solution.py:339
  112.2 0.0 copy-done.8
  112.2 0.0 copy-done.9
  112.2 0.0 copy-done.11
  112.2 0.0 copy-start.2
  112.2 2.9 %copy-done.2 = f32[7,8,80,320]{3,2,1,0:T(8,128)S(1)} copy-done((f32[7,8,80,320]{3,2,1,0:T(8,128)S(1)}, f32[7,8,80,320]{3,2,1,0:T(8,128)}, u32[]{:S(2)}) %copy-start.2) | copy-done | bytes 5734424
  115.2 2.7 %mean.1 = (f32[8,80,320]{2,1,0:T(8,128)S(1)}, f32[24,324]{1,0:T(8,128)}) custom-call(s32[24]{0:T(128)S(1)} %copy-done.11, s32[1]{0:T(128)S(6)} %copy.17.count_ref, f32[8,128]{1,0:T(8,128)S(1)} %get-tuple-element.7.weights_ref, f32[7,8,80,320]{3,2,1,0:T(8,128)S(1)} %copy-done.2, f32[7,24,324]{2,1,0:T(8,128)S(1)} %copy-done.9, f32[7,24,324]{2,1,0:T(8,128)S(1)} %copy-done.8), custom_call_target="tpu_custom_call" | custom-call | tf_op jit(solution)/shard_map/mean/pallas_call | solution.py:348
  117.8 18.0 %all-to-all-done.4 = f32[64,25,1,128]{3,2,1,0:T(1,128)S(1)} async-done(((f32[64,25,1,128]{3,2,1,0:T(1,128)}), f32[64,25,1,128]{3,2,1,0:T(1,128)S(1)}, u32[]{:S(2)}, u32[]{:S(2)}) %all-to-all-start.4) | async-done | bytes 819232 | tf_op jit(solution)/shard_map/all_to_all | solution.py:339
  135.8 2.2 %x_inverse.1 = f32[8,80,320]{2,1,0:T(8,128)} custom-call(f32[1600,128]{1,0:T(8,128)S(1)} %bitcast.10, f32[8,80,320]{2,1,0:T(8,128)S(1)} %get-tuple-element.8.mean_ref, bf16[320,320]{1,0:T(8,128)(2,1)S(1)} %copy-done.4, bf16[320,320]{1,0:T(8,128)(2,1)S(1)} %copy-done.3), custom_call_target="tpu_custom_call" | custom-call | tf_op jit(solution)/shard_map/x_inverse/pallas_call | solution.py:396
Async XLA Ops:
  1.3 3.0 %copy-start = (f32[7,8,80,320]{3,2,1,0:T(8,128)S(1)}, f32[7,8,80,320]{3,2,1,0:T(8,128)}, u32[]{:S(2)}) copy-start(f32[7,8,80,320]{3,2,1,0:T(8,128)} %residual_ref.3) | copy-start | bytes 17203204
  4.2 0.9 copy-start.7
  5.2 0.7 copy-start.10
  5.8 31.7 %copy-start.1 = (f32[7,8,80,320]{3,2,1,0:T(8,128)S(1)}, f32[7,8,80,320]{3,2,1,0:T(8,128)}, u32[]{:S(2)}) copy-start(f32[7,8,80,320]{3,2,1,0:T(8,128)} %residual_ref.3) | copy-start | bytes 17203204
  5.8 31.7 %copy-start.3 = (bf16[320,320]{1,0:T(8,128)(2,1)S(1)}, bf16[320,320]{1,0:T(8,128)(2,1)}, u32[]{:S(2)}) copy-start(bf16[320,320]{1,0:T(8,128)(2,1)} %constant.30.clone.low_ref) | copy-start | bytes 614404
  5.8 31.7 %copy-start.4 = (bf16[320,320]{1,0:T(8,128)(2,1)S(1)}, bf16[320,320]{1,0:T(8,128)(2,1)}, u32[]{:S(2)}) copy-start(bf16[320,320]{1,0:T(8,128)(2,1)} %constant.29.clone.high_ref) | copy-start | bytes 614404
  5.8 62.6 %copy-start.5 = (bf16[512,512]{1,0:T(8,128)(2,1)S(1)}, bf16[512,512]{1,0:T(8,128)(2,1)}, u32[]{:S(2)}) copy-start(bf16[512,512]{1,0:T(8,128)(2,1)} %constant.32.clone.low_ref) | copy-start | bytes 1572868
  5.8 62.6 %copy-start.6 = (bf16[512,512]{1,0:T(8,128)(2,1)S(1)}, bf16[512,512]{1,0:T(8,128)(2,1)}, u32[]{:S(2)}) copy-start(bf16[512,512]{1,0:T(8,128)(2,1)} %constant.31.clone.high_ref) | copy-start | bytes 1572868
  40.2 71.9 %copy-start.8 = (f32[7,24,324]{2,1,0:T(8,128)S(1)}, f32[7,24,324]{2,1,0:T(8,128)}, u32[]{:S(2)}) copy-start(f32[7,24,324]{2,1,0:T(8,128)} %block_residual_ref.1) | copy-start | bytes 653188
  40.2 71.9 %copy-start.9 = (f32[7,24,324]{2,1,0:T(8,128)S(1)}, f32[7,24,324]{2,1,0:T(8,128)}, u32[]{:S(2)}) copy-start(f32[7,24,324]{2,1,0:T(8,128)} %block_ref.3) | copy-start | bytes 653188
  40.3 71.9 %copy-start.11 = (s32[24]{0:T(128)S(1)}, s32[24]{0:T(128)}, u32[]{:S(2)}) copy-start(s32[24]{0:T(128)} %species_ref.3) | copy-start | bytes 292
  70.7 15.5 %all-to-all-start.2 = ((f32[4,400,128]{2,1,0:T(8,128)}), f32[4,400,128]{2,1,0:T(8,128)S(1)}, u32[]{:S(2)}, u32[]{:S(2)}) async-start(f32[4,400,128]{2,1,0:T(8,128)} %z_forward.1), calls=%async_computation.2 | async-start | bytes 1638400 | tf_op jit(solution)/shard_map/all_to_all | solution.py:344
  104.0 31.8 %all-to-all-start.4 = ((f32[64,25,1,128]{3,2,1,0:T(1,128)}), f32[64,25,1,128]{3,2,1,0:T(1,128)S(1)}, u32[]{:S(2)}, u32[]{:S(2)}) async-start(f32[64,25,1,128]{3,2,1,0:T(1,128)} %bitcast.7), calls=%async_computation.4 | async-start | bytes 1638400 | tf_op jit(solution)/shard_map/all_to_all | solution.py:339
  112.2 3.0 %copy-start.2 = (f32[7,8,80,320]{3,2,1,0:T(8,128)S(1)}, f32[7,8,80,320]{3,2,1,0:T(8,128)}, u32[]{:S(2)}) copy-start(f32[7,8,80,320]{3,2,1,0:T(8,128)} %density_ref.1) | copy-start | bytes 17203204
where the time goes:
time: 138 us
  blocking collectives  69.7 us (51%)
  waiting for transfers between devices  29.9 us (22%)
  Pallas kernels  17.8 us (13%)
  starting transfers between devices  11.6 us (8%)
  local copies, waits for them, and re-layouts  7.54 us (5%)
  between operations  1.41 us (1%)
    all_to_all x1, blocking collectives, body(): lax.all_to_all(sums.reshape(devices, 1, LANES), SLAB_PENCIL, split_axis=0...  28.2 us
    all_to_all x1, blocking collectives, slab_move(): lax.all_to_all(array.reshape(shape), SLAB, split_axis=0, concat_axis=0, t...  28.2 us
    all_to_all x1, waiting for transfers between devices, slab_move(): lax.all_to_all(array.reshape(shape), SLAB, split_axis=0, concat_axis=0, t...  18 us
    all_to_all x1, blocking collectives, pencil_move(): lax.all_to_all(array, 'pencil', split_axis=0, concat_axis=0, tiled=True)  13.2 us
    all_to_all x1, waiting for transfers between devices, pencil_move(): lax.all_to_all(array, 'pencil', split_axis=0, concat_axis=0, tiled=True)  11.9 us
    all_to_all x1, starting transfers between devices, slab_move(): lax.all_to_all(array.reshape(shape), SLAB, split_axis=0, concat_axis=0, t...  8.12 us
    unnamed x24, local copies, waits for them, and re-layouts  7.54 us
    all_to_all x1, starting transfers between devices, pencil_move(): lax.all_to_all(array, 'pencil', split_axis=0, concat_axis=0, tiled=True)  3.5 us
  transfers between devices with their start and end apart: 2, of which 2 were waited for; matrix products, arithmetic and copies ran while one was open for 0% of the time, Pallas kernels for 2%

commit v1 on v0

v1 whole, which is shorter than its diff:
```python
import functools
import math

import jax
import jax.numpy as jnp
import numpy as np
from jax import lax
from jax.experimental import pallas as pl
from jax.experimental.pallas import tpu as pltpu
from jax.sharding import Mesh
from jax.sharding import PartitionSpec as P

ORBITALS = 18
SLAB = ("slab_0", "slab_1", "slab_2")
SLAB_PENCIL = ("slab_0", "slab_1", "slab_2", "pencil")

grid_mixing = 0.5
block_mixing = 0.5
kerker_wave = 6.0
species_orbitals = (18, 13, 8, 5)

f32 = jnp.float32
bf16 = jnp.bfloat16
LANES = 128
MIB = 1 << 20


def pair_list(histories):
    return [(i, j) for i in range(histories) for j in range(i, histories)]


def split(value):
    high = value.astype(bf16)
    return high, (value - high.astype(f32)).astype(bf16)


def product(left, right, dims):
    dot = functools.partial(
        lax.dot_general, dimension_numbers=(dims, ((), ())), preferred_element_type=f32
    )
    return dot(left[0], right[0]) + (dot(left[0], right[1]) + dot(left[1], right[0]))


def hartley(rows, columns, length):
    angle = (np.outer(rows, columns) % length) * (2.0 * math.pi / length)
    table = np.cos(angle) + np.sin(angle)
    high = table.astype(bf16)
    low = (table - high.astype(np.float64)).astype(bf16)
    return high, low


def block_mask(species_ref, count_ref, slots, entries):
    row = lax.broadcasted_iota(jnp.int32, (slots, entries), 0)
    entry = lax.broadcasted_iota(jnp.int32, (slots, entries), 1)
    row_index = (entry * 3641) >> 16
    column_index = entry - ORBITALS * row_index
    limit = jnp.zeros((slots, entries), jnp.int32)
    for slot in range(slots):
        kind = species_ref[slot]
        number = jnp.int32(0)
        for index, orbital_number in enumerate(species_orbitals):
            number = jnp.where(kind == index, jnp.int32(orbital_number), number)
        number = jnp.where(slot < count_ref[0], number, jnp.int32(0))
        limit = jnp.where(row == slot, number, limit)
    return (row_index < limit) & (column_index < limit)


def gram_kernel(
    species_ref,
    count_ref,
    residual_ref,
    block_ref,
    out_ref,
    held_ref,
    acc_ref,
    arrived,
    *,
    cell_total,
    block_total,
):
    histories, planes, rows, width = residual_ref.shape
    pairs = pair_list(histories)

    def fetch(z):
        return pltpu.make_async_copy(residual_ref.at[:, z], held_ref.at[:, z], arrived.at[z])

    for z in range(planes):
        fetch(z).start()
    acc_ref[...] = jnp.zeros_like(acc_ref)
    _, slots, entries = block_ref.shape
    mask = block_mask(species_ref, count_ref, slots, entries)
    blocks = [jnp.where(mask, block_ref[i], 0.0) for i in range(histories)]
    lane = lax.broadcasted_iota(jnp.int32, (1, LANES), 1)
    line = jnp.zeros((1, LANES), f32)
    for k, (i, j) in enumerate(pairs):
        block_part = jnp.sum(blocks[i] * blocks[j], axis=(0, 1), keepdims=True) / block_total
        line = jnp.where(lane == k, block_part, line)

    def plane(z, carry):
        fetch(z).wait()
        for start in range(0, width, LANES):
            lanes = slice(start, min(start + LANES, width))
            accs = [acc_ref[k, :, lanes] for k in range(len(pairs))]
            for top in range(0, rows, 8):
                values = [held_ref[i, z, top : top + 8, lanes] for i in range(histories)]
                accs = [acc + values[i] * values[j] for acc, (i, j) in zip(accs, pairs)]
            for k, acc in enumerate(accs):
                acc_ref[k, :, lanes] = acc
        return carry

    lax.fori_loop(0, planes, plane, 0)
    for k in range(len(pairs)):
        grid_part = jnp.sum(acc_ref[k], axis=(0, 1), keepdims=True) / cell_total
        line = jnp.where(lane == k, line + grid_part, line)
    out_ref[...] = jnp.broadcast_to(line, out_ref.shape)


def mixing_weights(line, histories):
    lane = lax.broadcasted_iota(jnp.int32, (1, LANES), 1)
    entry = {}
    for k, (i, j) in enumerate(pair_list(histories)):
        entry[j, i] = jnp.sum(jnp.where(lane == k, line, 0.0), axis=1, keepdims=True)
    factor = {}
    inverse = {}
    work = dict(entry)
    for k in range(histories):
        inverse[k] = 1.0 / work[k, k]
        for i in range(k + 1, histories):
            factor[i, k] = work[i, k] * inverse[k]
        for i in range(k + 1, histories):
            for j in range(k + 1, i + 1):
                work[i, j] = work[i, j] - factor[i, k] * work[j, k]
    solved = [jnp.ones((1, 1), f32) for _ in range(histories)]
    for i in range(histories):
        for k in range(i):
            solved[i] = solved[i] - factor[i, k] * solved[k]
    solved = [value * inverse[i] for i, value in enumerate(solved)]
    for i in reversed(range(histories)):
        for k in range(i + 1, histories):
            solved[i] = solved[i] - factor[k, i] * solved[k]
    total = solved[0]
    for value in solved[1:]:
        total = total + value
    return [value / total for value in solved]


def mix_kernel(
    sums_ref, residual_ref, high_ref, low_ref, out_ref, weights_ref, mixed_high, mixed_low, *, slab_count
):
    histories, planes, rows, _ = residual_ref.shape
    line = jnp.sum(sums_ref[...], axis=0, keepdims=True)
    weights = mixing_weights(line, histories)
    for i, weight in enumerate(weights):
        weights_ref[i : i + 1, :] = jnp.broadcast_to(weight, (1, LANES))
    weights_ref[histories:, :] = jnp.zeros((8 - histories, LANES), f32)
    for z in range(planes):
        mixed = weights[0] * residual_ref[0, z]
        for i in range(1, histories):
            mixed = mixed + weights[i] * residual_ref[i, z]
        high, low = split(mixed)
        mixed_high[z * rows : (z + 1) * rows, :] = high
        mixed_low[z * rows : (z + 1) * rows, :] = low
    table = (high_ref[...], low_ref[...])
    result = product(table, (mixed_high[...], mixed_low[...]), ((1,), (1,)))
    pieces = result.shape[1] // LANES
    own_planes = result.shape[0] // slab_count - 1
    message = out_ref.shape[0] // (slab_count * own_planes)
    period = own_planes * message
    extra = message - pieces

    def put(row, plane, piece):
        out_ref[pl.ds(row, slab_count, stride=period), :] = result[
            plane * slab_count : (plane + 1) * slab_count, piece * LANES : (piece + 1) * LANES
        ]

    for own in range(own_planes):
        for piece in range(pieces):
            put(own * message + piece, own, piece)
        first = (pieces - extra) * (own // 2)
        for piece in range(extra):
            put(own * message + pieces + piece, own_planes, first + piece)


def plane_kernel(
    place_ref,
    in_ref,
    zh_ref,
    zl_ref,
    yh_ref,
    yl_ref,
    out_ref,
    main_ref,
    half_ref,
    *,
    slab_count,
    pencil_count,
    z_local,
    y_local,
    x_length,
    scale,
):
    z_length = slab_count * z_local
    y_length = pencil_count * y_local
    message = in_ref.shape[0] // (slab_count * pencil_count)
    period = pencil_count * message
    pieces = z_local * y_local // LANES
    extra = message - pieces
    half = z_local // 2
    half_rows = half * y_local
    spare = pieces * LANES - half_rows - (pieces - extra) * LANES
    in_half = place_ref[1] // 2
    out_half = place_ref[1] % 2

    def taken(row):
        return in_ref[pl.ds(row, slab_count, stride=period), :].T

    def spread(rows, count):
        return jnp.concatenate([rows[z * y_local : (z + 1) * y_local] for z in range(count)], axis=1)

    def stacked(block, count):
        return jnp.concatenate(
            [block[:, z * slab_count : (z + 1) * slab_count] for z in range(count)], axis=0
        )

    for q in range(pencil_count):
        here = slice(q * y_local, (q + 1) * y_local)
        rows = jnp.concatenate([taken(q * message + k) for k in range(pieces)], axis=0)
        main_ref[here, :] = spread(rows, z_local)
        rows = jnp.concatenate([taken(q * message + pieces + k) for k in range(extra)], axis=0)
        rows = jnp.where(in_half == 0, rows[:half_rows], rows[spare : spare + half_rows])
        half_ref[here, :] = spread(rows, half)

    z_table = (zh_ref[...], zl_ref[...])
    y_table = (yh_ref[...], yl_ref[...])

    def half_table(which):
        rows = pl.ds(pl.multiple_of(which * (z_length // 2), LANES), z_length // 2)
        return (zh_ref[rows, :], zl_ref[rows, :])

    lines = jnp.concatenate(
        [
            product(split(main_ref[...]), z_table, ((1,), (0,))),
            product(split(half_ref[...]), half_table(in_half), ((1,), (0,))),
        ],
        axis=1,
    )
    spectrum = product(y_table, split(lines), ((1,), (0,)))
    freq_y = lax.broadcasted_iota(jnp.int32, (y_length, z_length), 0)
    freq_z = lax.broadcasted_iota(jnp.int32, (y_length, z_length), 1)
    mag_y = jnp.minimum(freq_y, y_length - freq_y).astype(f32)
    mag_z = jnp.minimum(freq_z, z_length - freq_z).astype(f32)
    plane = mag_y * mag_y + mag_z * mag_z
    kept = []
    for j, own in enumerate((place_ref[1], pencil_count)):
        freq_x = place_ref[0] * (pencil_count + 1) + own
        mag_x = jnp.minimum(freq_x, x_length - freq_x).astype(f32)
        square = plane + mag_x * mag_x
        factor = square / (square + kerker_wave * kerker_wave) * scale
        kept.append(spectrum[:, j * z_length : (j + 1) * z_length] * factor)
    kept = product(y_table, split(jnp.concatenate(kept, axis=1)), ((1,), (0,)))
    main = product(split(kept[:, :z_length]), z_table, ((1,), (1,)))
    part = product(split(kept[:, z_length:]), half_table(out_half), ((1,), (1,)))
    filler = jnp.zeros((extra * LANES - half_rows, slab_count), f32)
    for q in range(pencil_count):
        here = slice(q * y_local, (q + 1) * y_local)
        rows = jnp.concatenate([stacked(main[here], z_local), stacked(part[here], half), filler], axis=0)
        for k in range(message):
            out_ref[pl.ds(q * message + k, slab_count, stride=period), :] = rows[
                k * LANES : (k + 1) * LANES
            ].T


def mean_kernel(
    species_ref, count_ref, weights_ref, density_ref, block_ref, block_residual_ref, out_ref, out_block_ref
):
    step = pl.program_id(0)
    histories = density_ref.shape[0]
    weights = [weights_ref[i : i + 1, 0:1] for i in range(histories)]
    mean = weights[0] * density_ref[0, 0]
    for i in range(1, histories):
        mean = mean + weights[i] * density_ref[i, 0]
    out_ref[0] = mean

    @pl.when(step == 0)
    def _():
        _, slots, entries = block_ref.shape
        mask = block_mask(species_ref, count_ref, slots, entries)
        total = weights[0] * (block_ref[0] + block_mixing * block_residual_ref[0])
        for i in range(1, histories):
            total = total + weights[i] * (block_ref[i] + block_mixing * block_residual_ref[i])
        out_block_ref[...] = jnp.where(mask, total, 0.0)


def x_inverse_kernel(
    in_ref, mean_ref, high_ref, low_ref, out_ref, field_ref, sent, *, slab_count, pencil_count
):
    rows, x_length = mean_ref.shape
    table = (high_ref[...], low_ref[...])
    pieces = rows // LANES
    message = in_ref.shape[0] // (slab_count * pencil_count)

    def taken(row):
        return in_ref[pl.ds(row, slab_count, stride=pencil_count * message), :]

    halves = []
    for out_half in range(2):
        parts = [
            taken(out_half * message + k) + taken((out_half + 2) * message + k)
            for k in range(pieces, message)
        ]
        halves.append(jnp.concatenate(parts, axis=1)[:, : rows // 2])
    shared = jnp.concatenate(halves, axis=1)

    def send(piece):
        here = pl.ds(piece * LANES, LANES)
        return pltpu.make_async_copy(field_ref.at[here], out_ref.at[here], sent.at[piece])

    for piece in range(pieces):
        here = slice(piece * LANES, (piece + 1) * LANES)
        block = [taken(q * message + piece) for q in range(pencil_count)]
        block.append(shared[:, here])
        field = product(split(jnp.concatenate(block, axis=0).T), table, ((1,), (0,)))
        field_ref[here, :] = mean_ref[here, :] + field
        send(piece).start()
    for piece in range(pieces):
        send(piece).wait()


def whole():
    return pl.BlockSpec(memory_space=pltpu.VMEM)


def scalars():
    return pl.BlockSpec(memory_space=pltpu.SMEM)


def in_hbm(array):
    return pltpu.with_memory_space_constraint(array, pltpu.HBM)


def params(limit):
    return pltpu.CompilerParams(vmem_limit_bytes=limit * MIB)


def body(
    density_history, residual_history, occupancy_history, occupancy_residual, species, slot_count
):
    histories, z_local, y_local, x_length = residual_history.shape
    slab_count = lax.axis_size(SLAB)
    pencil_count = lax.axis_size("pencil")
    devices = slab_count * pencil_count
    y_length = y_local * pencil_count
    z_length = z_local * slab_count
    slots, entries = occupancy_residual.shape[1:]
    kx_local = x_length // slab_count
    message = z_local * y_local // LANES + -(-z_local * y_local // (2 * LANES))
    rows = devices * message
    cell_total = float(z_length * y_length * x_length)
    x_order = (np.arange(slab_count)[None, :] * kx_local + np.arange(kx_local)[:, None]).reshape(-1)
    x_table = hartley(x_order, np.arange(x_length), x_length)
    y_table = hartley(np.arange(y_length), np.arange(y_length), y_length)
    z_order = (np.arange(slab_count)[None, :] * z_local + np.arange(z_local)[:, None]).reshape(-1)
    z_table = hartley(z_order, np.arange(z_length), z_length)
    place = jnp.stack([lax.axis_index(SLAB), lax.axis_index("pencil")]).astype(jnp.int32)
    place, species = lax.optimization_barrier((place, species))

    sums, held = pl.pallas_call(
        functools.partial(
            gram_kernel, cell_total=cell_total, block_total=100.0 * slots * devices
        ),
        in_specs=[scalars(), scalars(), pl.BlockSpec(memory_space=pltpu.HBM), whole()],
        out_specs=[whole(), whole()],
        out_shape=[
            jax.ShapeDtypeStruct((devices, LANES), f32),
            jax.ShapeDtypeStruct(residual_history.shape, f32),
        ],
        scratch_shapes=[
            pltpu.VMEM((len(pair_list(histories)), 8, x_length), f32),
            pltpu.SemaphoreType.DMA((z_local,)),
        ],
        compiler_params=params(16),
        name="gram",
    )(in_hbm(species), slot_count, in_hbm(residual_history), in_hbm(occupancy_residual))

    def exchange(array):
        return lax.all_to_all(
            array.reshape(devices, -1, 1, LANES), SLAB_PENCIL, split_axis=0, concat_axis=0, tiled=True
        ).reshape(-1, LANES)

    sums = exchange(sums)
    packed, weights = pl.pallas_call(
        functools.partial(mix_kernel, slab_count=slab_count),
        in_specs=[whole()] * 4,
        out_specs=[whole(), whole()],
        out_shape=[
            jax.ShapeDtypeStruct((rows, LANES), f32),
            jax.ShapeDtypeStruct((8, LANES), f32),
        ],
        scratch_shapes=[
            pltpu.VMEM((z_local * y_local, x_length), bf16),
            pltpu.VMEM((z_local * y_local, x_length), bf16),
        ],
        compiler_params=params(24),
        name="mix",
    )(sums, held, *x_table)
    moved = exchange(packed)
    plane_in = pl.BlockSpec((histories, 1, y_local, x_length), lambda z: (0, z, 0, 0))
    mean, new_occupancy = pl.pallas_call(
        mean_kernel,
        grid=(z_local,),
        in_specs=[scalars(), scalars(), whole(), plane_in, whole(), whole()],
        out_specs=[pl.BlockSpec((1, y_local, x_length), lambda z: (z, 0, 0)), whole()],
        out_shape=[
            jax.ShapeDtypeStruct((z_local, y_local, x_length), f32),
            jax.ShapeDtypeStruct((slots, entries), f32),
        ],
        compiler_params=params(16),
        name="mean",
    )(species, slot_count, weights, density_history, occupancy_history, occupancy_residual)
    packed = pl.pallas_call(
        functools.partial(
            plane_kernel,
            slab_count=slab_count,
            pencil_count=pencil_count,
            z_local=z_local,
            y_local=y_local,
            x_length=x_length,
            scale=grid_mixing / cell_total,
        ),
        in_specs=[scalars()] + [whole()] * 5,
        out_specs=whole(),
        out_shape=jax.ShapeDtypeStruct((rows, LANES), f32),
        scratch_shapes=[
            pltpu.VMEM((y_length, z_length), f32),
            pltpu.VMEM((y_length, z_length // 2), f32),
        ],
        compiler_params=params(32),
        name="plane",
    )(place, moved, *z_table, *y_table)
    moved = exchange(packed)
    new_density = pl.pallas_call(
        functools.partial(x_inverse_kernel, slab_count=slab_count, pencil_count=pencil_count),
        in_specs=[whole()] * 4,
        out_specs=pl.BlockSpec(memory_space=pltpu.HBM),
        out_shape=jax.ShapeDtypeStruct((z_local * y_local, x_length), f32),
        scratch_shapes=[
            pltpu.VMEM((z_local * y_local, x_length), f32),
            pltpu.SemaphoreType.DMA((z_local * y_local // LANES,)),
        ],
        compiler_params=params(24),
        name="x_inverse",
    )(moved, mean.reshape(z_local * y_local, x_length), *x_table)
    return (new_density.reshape(z_local, y_local, x_length), new_occupancy)


def solution(mesh):
    torus = Mesh(
        mesh.devices.reshape(8, 4, 2, mesh.shape["pencil"]),
        ("slab_0", "slab_1", "slab_2", "pencil"),
    )
    placed = (
        P(None, SLAB, "pencil", None),
        P(None, SLAB, "pencil", None),
        P(None, SLAB_PENCIL, None),
        P(None, SLAB_PENCIL, None),
        P(SLAB_PENCIL),
        P(SLAB_PENCIL),
    )
    return jax.shard_map(
        body,
        mesh=torus,
        in_specs=placed,
        out_specs=(P(SLAB, "pencil", None), P(SLAB_PENCIL, None)),
        check_vma=False,
    )
```

time: 138 us -> 120 us (0.87)
  blocking collectives: 69.7 us -> 64.6 us
  starting transfers between devices: 11.6 us -> 6.61 us
  waiting for transfers between devices: 29.9 us -> 25.2 us
  local copies, waits for them, and re-layouts: 7.54 us -> 2.99 us
    all_to_all x3 -> x2, blocking collectives: 69.7 us -> 64.6 us  [exchange(): lax.all_to_all(array.reshape(devices, -1, 1, LANES), SLAB_PENCIL, split_a...]
    all_to_all x2 -> x1, starting transfers between devices: 11.6 us -> 6.61 us  [exchange(): lax.all_to_all(array.reshape(devices, -1, 1, LANES), SLAB_PENCIL, split_a...]
    all_to_all x2 -> x1, waiting for transfers between devices: 29.9 us -> 25.2 us  [exchange(): lax.all_to_all(array.reshape(devices, -1, 1, LANES), SLAB_PENCIL, split_a...]
    unnamed x24 -> x20, local copies, waits for them, and re-layouts: 7.54 us -> 2.99 us
    pallas_call x5 -> x3, Pallas kernels: 11.8 us -> 11.5 us  [the longest x1 7.16 us: body(): pl.pallas_call(functools.partial(plane_kernel, slab_count=slab_count, pen...]
  transfers between devices with their start and end apart: 2 -> 1, of which waited for: 2 -> 1; matrix products, arithmetic and copies ran while one was open for 0% -> 0% of each run, Pallas kernels for 2% -> 2%
where the time goes in v1:
time: 120 us
  blocking collectives  64.6 us (54%)
  waiting for transfers between devices  25.2 us (21%)
  Pallas kernels  18.8 us (16%)
  starting transfers between devices  6.61 us (6%)
  local copies, waits for them, and re-layouts  2.99 us (2%)
  between operations  1.45 us (1%)
    all_to_all x2, blocking collectives, exchange(): lax.all_to_all(array.reshape(devices, -1, 1, LANES), SLAB_PENCIL, split_a...  64.6 us
    all_to_all x1, waiting for transfers between devices, exchange(): lax.all_to_all(array.reshape(devices, -1, 1, LANES), SLAB_PENCIL, split_a...  25.2 us
    pallas_call x1, Pallas kernels, body(): pl.pallas_call(functools.partial(plane_kernel, slab_count=slab_count, pen...  7.16 us
    all_to_all x1, starting transfers between devices, exchange(): lax.all_to_all(array.reshape(devices, -1, 1, LANES), SLAB_PENCIL, split_a...  6.61 us
    pallas_call x1, Pallas kernels, body(): pl.pallas_call(functools.partial(gram_kernel, cell_total=cell_total, bloc...  4.59 us
    unnamed x20, local copies, waits for them, and re-layouts  2.99 us
    pallas_call x1, Pallas kernels, body(): pl.pallas_call(mean_kernel, grid=(z_local,), in_specs=[scalars(), scalars...  2.67 us
  transfers between devices with their start and end apart: 1, of which 1 were waited for; matrix products, arithmetic and copies ran while one was open for 0% of the time, Pallas kernels for 2%

profile of v1, /device:TPU:1, one launch (start us, length us, event | category | flops | bytes accessed | tf_op | source)
XLA Modules:
  0.0 119.7 jit_solution(2052481219575984838)
XLA Ops:
  0.6 0.0 copy-start.2
  0.6 0.0 copy-start.3
  1.4 0.1 pad_add_fusion.place_ref
  1.4 0.0 copy-start.4
  1.4 0.0 copy-start.5
  1.4 0.0 copy-start.7
  1.4 0.0 copy-start.8
  1.4 4.6 %gram.1 = (f32[256,128]{1,0:T(8,128)S(1)}, f32[7,8,80,320]{3,2,1,0:T(8,128)S(1)}) custom-call(s32[24]{0:T(128)} %species_ref.1, s32[1]{0:T(128)S(6)} %copy.17.count_ref, f32[7,8,80,320]{3,2,1,0:T(8,128)} %residual_ref.1, f32[7,24,324]{2,1,0:T(8,128)} %block_residual_ref.1), custom_call_target="tpu_custom_call" | custom-call | tf_op jit(solution)/shard_map/gram/pallas_call | solution.py:367
  6.1 28.2 %all_to_all.15 = f32[256,1,1,128]{3,2,1,0:T(1,128)S(1)} all-to-all(f32[256,1,1,128]{3,2,1,0:T(1,128)S(1)} %bitcast.21), channel_id=1, replica_groups=mesh['slab_0'=8,'slab_1'=4,'slab_2'=2,'pencil'=4] {'slab_0','slab_1','sl..., dimensions={0} | all-to-all | bytes 262144 | tf_op jit(solution)/shard_map/all_to_all | solution.py:386
  34.3 0.0 copy-done.2
  34.3 0.0 copy-done.3
  34.3 0.0 copy-start.1
  34.3 0.0 copy-start.6
  34.3 0.0 copy-start.9
  34.3 2.0 %mix.1 = (f32[2048,128]{1,0:T(8,128)S(1)}, f32[8,128]{1,0:T(8,128)S(1)}) custom-call(f32[256,128]{1,0:T(8,128)S(1)} %bitcast.20, f32[7,8,80,320]{3,2,1,0:T(8,128)S(1)} %get-tuple-element.13.residual_ref, bf16[320,320]{1,0:T(8,128)(2,1)S(1)} %copy-done.3, bf16[320,320]{1,0:T(8,128)(2,1)S(1)} %copy-done.2), custom_call_target="tpu_custom_call" | custom-call | tf_op jit(solution)/shard_map/mix/pallas_call | solution.py:391
  36.4 36.3 %all_to_all.16 = f32[256,8,1,128]{3,1,2,0:T(8,128)S(1)} all-to-all(f32[256,8,1,128]{3,1,2,0:T(8,128)S(1)} %bitcast.18), channel_id=1, replica_groups=mesh['slab_0'=8,'slab_1'=4,'slab_2'=2,'pencil'=4] {'slab_0','slab_1','sl..., dimensions={0} | all-to-all | bytes 2097152 | tf_op jit(solution)/shard_map/all_to_all | solution.py:386
  72.7 0.0 copy-done.4
  72.7 0.0 copy-done.5
  72.7 0.0 copy-done.7
  72.7 0.0 copy-done.8
  72.7 7.2 %plane.1 = f32[2048,128]{1,0:T(8,128)} custom-call(s32[2]{0:T(128)S(1)} %pad_add_fusion.place_ref, f32[2048,128]{1,0:T(8,128)S(1)} %bitcast.17, bf16[512,512]{1,0:T(8,128)(2,1)S(1)} %copy-done.5, bf16[512,512]{1,0:T(8,128)(2,1)S(1)} %copy-done.4, bf16[320,320]{1,0:T(8,128)(2,1)S(1)} %copy-done.8, bf16[320,320]{1,0:T(8,128)(2,1)S(1)} %copy-done.7), custom_call_target="tpu_custom_call" | custom-call | tf_op jit(solution)/shard_map/plane/pallas_call | solution.py:420
  79.9 6.6 %all-to-all-start.2 = ((f32[256,8,1,128]{3,1,2,0:T(8,128)}), f32[256,8,1,128]{3,1,2,0:T(8,128)S(1)}, u32[]{:S(2)}, u32[]{:S(2)}) async-start(f32[256,8,1,128]{3,1,2,0:T(8,128)} %bitcast.9), calls=%async_computation.2 | async-start | bytes 2097152 | tf_op jit(solution)/shard_map/all_to_all | solution.py:386
  86.5 0.0 copy-done.1
  86.5 0.0 copy-done.6
  86.5 0.0 copy-done.9
  86.5 0.0 copy-start
  86.6 2.9 %copy-done = f32[7,8,80,320]{3,2,1,0:T(8,128)S(1)} copy-done((f32[7,8,80,320]{3,2,1,0:T(8,128)S(1)}, f32[7,8,80,320]{3,2,1,0:T(8,128)}, u32[]{:S(2)}) %copy-start) | copy-done | bytes 5734424
  89.5 2.7 %mean.1 = (f32[8,80,320]{2,1,0:T(8,128)S(1)}, f32[24,324]{1,0:T(8,128)}) custom-call(s32[24]{0:T(128)S(1)} %copy-done.9, s32[1]{0:T(128)S(6)} %copy.17.count_ref, f32[8,128]{1,0:T(8,128)S(1)} %get-tuple-element.15.weights_ref, f32[7,8,80,320]{3,2,1,0:T(8,128)S(1)} %copy-done, f32[7,24,324]{2,1,0:T(8,128)S(1)} %copy-done.6, f32[7,24,324]{2,1,0:T(8,128)S(1)} %copy-done.1), custom_call_target="tpu_custom_call" | custom-call | tf_op jit(solution)/shard_map/mean/pallas_call | solution.py:408
  92.2 25.2 %all-to-all-done.2 = f32[256,8,1,128]{3,1,2,0:T(8,128)S(1)} async-done(((f32[256,8,1,128]{3,1,2,0:T(8,128)}), f32[256,8,1,128]{3,1,2,0:T(8,128)S(1)}, u32[]{:S(2)}, u32[]{:S(2)}) %all-to-all-start.2) | async-done | bytes 1048608 | tf_op jit(solution)/shard_map/all_to_all | solution.py:386
  117.4 2.3 %x_inverse.1 = f32[640,320]{1,0:T(8,128)} custom-call(f32[2048,128]{1,0:T(8,128)S(1)} %bitcast.16, f32[640,320]{1,0:T(8,128)S(1)} %bitcast.19, bf16[320,320]{1,0:T(8,128)(2,1)S(1)} %copy-done.3, bf16[320,320]{1,0:T(8,128)(2,1)S(1)} %copy-done.2), custom_call_target="tpu_custom_call" | custom-call | tf_op jit(solution)/shard_map/x_inverse/pallas_call | solution.py:441
Async XLA Ops:
  0.6 33.7 %copy-start.2 = (bf16[320,320]{1,0:T(8,128)(2,1)S(1)}, bf16[320,320]{1,0:T(8,128)(2,1)}, u32[]{:S(2)}) copy-start(bf16[320,320]{1,0:T(8,128)(2,1)} %constant.34.clone.low_ref) | copy-start | bytes 614404
  0.6 33.7 %copy-start.3 = (bf16[320,320]{1,0:T(8,128)(2,1)S(1)}, bf16[320,320]{1,0:T(8,128)(2,1)}, u32[]{:S(2)}) copy-start(bf16[320,320]{1,0:T(8,128)(2,1)} %constant.33.clone.high_ref) | copy-start | bytes 614404
  1.4 71.3 %copy-start.4 = (bf16[512,512]{1,0:T(8,128)(2,1)S(1)}, bf16[512,512]{1,0:T(8,128)(2,1)}, u32[]{:S(2)}) copy-start(bf16[512,512]{1,0:T(8,128)(2,1)} %constant.36.clone.zl_ref) | copy-start | bytes 1572868
  1.4 71.3 %copy-start.5 = (bf16[512,512]{1,0:T(8,128)(2,1)S(1)}, bf16[512,512]{1,0:T(8,128)(2,1)}, u32[]{:S(2)}) copy-start(bf16[512,512]{1,0:T(8,128)(2,1)} %constant.35.clone.zh_ref) | copy-start | bytes 1572868
  1.4 71.3 %copy-start.7 = (bf16[320,320]{1,0:T(8,128)(2,1)S(1)}, bf16[320,320]{1,0:T(8,128)(2,1)}, u32[]{:S(2)}) copy-start(bf16[320,320]{1,0:T(8,128)(2,1)} %constant.38.clone.yl_ref) | copy-start | bytes 614404
  1.4 71.3 %copy-start.8 = (bf16[320,320]{1,0:T(8,128)(2,1)S(1)}, bf16[320,320]{1,0:T(8,128)(2,1)}, u32[]{:S(2)}) copy-start(bf16[320,320]{1,0:T(8,128)(2,1)} %constant.37.clone.yh_ref) | copy-start | bytes 614404
  34.3 52.2 %copy-start.1 = (f32[7,24,324]{2,1,0:T(8,128)S(1)}, f32[7,24,324]{2,1,0:T(8,128)}, u32[]{:S(2)}) copy-start(f32[7,24,324]{2,1,0:T(8,128)} %block_residual_ref.1) | copy-start | bytes 653188
  34.3 52.2 %copy-start.6 = (f32[7,24,324]{2,1,0:T(8,128)S(1)}, f32[7,24,324]{2,1,0:T(8,128)}, u32[]{:S(2)}) copy-start(f32[7,24,324]{2,1,0:T(8,128)} %block_ref.3) | copy-start | bytes 653188
  34.3 52.2 %copy-start.9 = (s32[24]{0:T(128)S(1)}, s32[24]{0:T(128)}, u32[]{:S(2)}) copy-start(s32[24]{0:T(128)} %species_ref.1) | copy-start | bytes 292
  79.9 37.5 %all-to-all-start.2 = ((f32[256,8,1,128]{3,1,2,0:T(8,128)}), f32[256,8,1,128]{3,1,2,0:T(8,128)S(1)}, u32[]{:S(2)}, u32[]{:S(2)}) async-start(f32[256,8,1,128]{3,1,2,0:T(8,128)} %bitcast.9), calls=%async_computation.2 | async-start | bytes 2097152 | tf_op jit(solution)/shard_map/all_to_all | solution.py:386
  86.5 3.0 %copy-start = (f32[7,8,80,320]{3,2,1,0:T(8,128)S(1)}, f32[7,8,80,320]{3,2,1,0:T(8,128)}, u32[]{:S(2)}) copy-start(f32[7,8,80,320]{3,2,1,0:T(8,128)} %density_ref.1) | copy-start | bytes 17203204

commit v2 on v1

--- a/solution.py
+++ b/solution.py
@@ -63,6 +63,14 @@
         number = jnp.where(slot < count_ref[0], number, jnp.int32(0))
         limit = jnp.where(row == slot, number, limit)
     return (row_index < limit) & (column_index < limit)
+
+
+def parity_order(count):
+    return np.concatenate([np.arange(0, count, 2), np.arange(1, count, 2)])
+
+
+def parity_place(index, count):
+    return index // 2 + (index % 2) * (count // 2)
 
 
 def gram_kernel(
@@ -158,8 +166,9 @@
         for i in range(1, histories):
             mixed = mixed + weights[i] * residual_ref[i, z]
         high, low = split(mixed)
-        mixed_high[z * rows : (z + 1) * rows, :] = high
-        mixed_low[z * rows : (z + 1) * rows, :] = low
+        here = pl.ds(parity_place(z, planes) * rows, rows)
+        mixed_high[here, :] = high
+        mixed_low[here, :] = low
     table = (high_ref[...], low_ref[...])
     result = product(table, (mixed_high[...], mixed_low[...]), ((1,), (1,)))
     pieces = result.shape[1] // LANES
@@ -190,7 +199,7 @@
     yl_ref,
     out_ref,
     main_ref,
-    half_ref,
+    part_ref,
     *,
     slab_count,
     pencil_count,
@@ -201,6 +210,8 @@
 ):
     z_length = slab_count * z_local
     y_length = pencil_count * y_local
+    z_half = z_length // 2
+    y_half = y_length // 2
     message = in_ref.shape[0] // (slab_count * pencil_count)
     period = pencil_count * message
     pieces = z_local * y_local // LANES
@@ -217,53 +228,64 @@
     def spread(rows, count):
         return jnp.concatenate([rows[z * y_local : (z + 1) * y_local] for z in range(count)], axis=1)
 
-    def stacked(block, count):
-        return jnp.concatenate(
-            [block[:, z * slab_count : (z + 1) * slab_count] for z in range(count)], axis=0
-        )
-
     for q in range(pencil_count):
         here = slice(q * y_local, (q + 1) * y_local)
         rows = jnp.concatenate([taken(q * message + k) for k in range(pieces)], axis=0)
         main_ref[here, :] = spread(rows, z_local)
         rows = jnp.concatenate([taken(q * message + pieces + k) for k in range(extra)], axis=0)
         rows = jnp.where(in_half == 0, rows[:half_rows], rows[spare : spare + half_rows])
-        half_ref[here, :] = spread(rows, half)
-
-    z_table = (zh_ref[...], zl_ref[...])
-    y_table = (yh_ref[...], yl_ref[...])
-
-    def half_table(which):
-        rows = pl.ds(pl.multiple_of(which * (z_length // 2), LANES), z_length // 2)
+        part_ref[here, :] = spread(rows, half)
+
+    def z_table(which):
+        rows = pl.ds(pl.multiple_of(which * z_half, LANES), z_half)
         return (zh_ref[rows, :], zl_ref[rows, :])
 
-    lines = jnp.concatenate(
-        [
-            product(split(main_ref[...]), z_table, ((1,), (0,))),
-            product(split(half_ref[...]), half_table(in_half), ((1,), (0,))),
-        ],
-        axis=1,
-    )
-    spectrum = product(y_table, split(lines), ((1,), (0,)))
-    freq_y = lax.broadcasted_iota(jnp.int32, (y_length, z_length), 0)
+    even = product(split(main_ref[:, :z_half]), z_table(0), ((1,), (0,)))
+    odd = product(split(main_ref[:, z_half:]), z_table(1), ((1,), (0,)))
+    part = product(split(part_ref[...]), z_table(in_half), ((1,), (0,)))
+    lines = jnp.concatenate([even + odd, even - odd, part], axis=1)
+    even = product((yh_ref[0], yl_ref[0]), split(lines[:y_half] + lines[y_half:]), ((1,), (0,)))
+    odd = product((yh_ref[1], yl_ref[1]), split(lines[:y_half] - lines[y_half:]), ((1,), (0,)))
+    spectrum = jnp.concatenate([even, odd], axis=0)
+
+    row = lax.broadcasted_iota(jnp.int32, (y_length, z_length), 0)
+    freq_y = jnp.where(row < y_half, 2 * row, 2 * row - (y_length - 1))
     freq_z = lax.broadcasted_iota(jnp.int32, (y_length, z_length), 1)
     mag_y = jnp.minimum(freq_y, y_length - freq_y).astype(f32)
     mag_z = jnp.minimum(freq_z, z_length - freq_z).astype(f32)
     plane = mag_y * mag_y + mag_z * mag_z
-    kept = []
-    for j, own in enumerate((place_ref[1], pencil_count)):
+
+    def factor(own):
         freq_x = place_ref[0] * (pencil_count + 1) + own
         mag_x = jnp.minimum(freq_x, x_length - freq_x).astype(f32)
         square = plane + mag_x * mag_x
-        factor = square / (square + kerker_wave * kerker_wave) * scale
-        kept.append(spectrum[:, j * z_length : (j + 1) * z_length] * factor)
-    kept = product(y_table, split(jnp.concatenate(kept, axis=1)), ((1,), (0,)))
-    main = product(split(kept[:, :z_length]), z_table, ((1,), (1,)))
-    part = product(split(kept[:, z_length:]), half_table(out_half), ((1,), (1,)))
+        return square / (square + kerker_wave * kerker_wave) * scale
+
+    main = spectrum[:, :z_length] * factor(place_ref[1])
+    shared = factor(pencil_count)
+    same = jnp.where(in_half == out_half, 1.0, -1.0)
+    part = spectrum[:, z_length:] * (shared[:, :z_half] + same * shared[:, z_half:])
+    kept = jnp.concatenate(
+        [main[:, :z_half] + main[:, z_half:], main[:, :z_half] - main[:, z_half:], part], axis=1
+    )
+    even = product((yh_ref[0], yl_ref[0]), split(kept[:y_half]), ((1,), (0,)))
+    odd = product((yh_ref[2], yl_ref[2]), split(kept[y_half:]), ((1,), (0,)))
+    lines = jnp.concatenate([even + odd, even - odd], axis=0)
+    result = jnp.concatenate(
+        [
+            product(split(lines[:, :z_half]), z_table(0), ((1,), (1,))),
+            product(split(lines[:, z_half:z_length]), z_table(1), ((1,), (1,))),
+            product(split(lines[:, z_length:]), z_table(out_half), ((1,), (1,))),
+        ],
+        axis=1,
+    )
     filler = jnp.zeros((extra * LANES - half_rows, slab_count), f32)
     for q in range(pencil_count):
-        here = slice(q * y_local, (q + 1) * y_local)
-        rows = jnp.concatenate([stacked(main[here], z_local), stacked(part[here], half), filler], axis=0)
+        block = result[q * y_local : (q + 1) * y_local]
+        rows = [
+            block[:, z * slab_count : (z + 1) * slab_count] for z in range(z_local + half)
+        ]
+        rows = jnp.concatenate(rows + [filler], axis=0)
         for k in range(message):
             out_ref[pl.ds(q * message + k, slab_count, stride=period), :] = rows[
                 k * LANES : (k + 1) * LANES
@@ -292,12 +314,24 @@
 
 
 def x_inverse_kernel(
-    in_ref, mean_ref, high_ref, low_ref, out_ref, field_ref, sent, *, slab_count, pencil_count
+    in_ref,
+    mean_ref,
+    high_ref,
+    low_ref,
+    out_ref,
+    field_ref,
+    sent,
+    *,
+    slab_count,
+    pencil_count,
+    z_local,
 ):
     rows, x_length = mean_ref.shape
+    y_local = rows // z_local
     table = (high_ref[...], low_ref[...])
     pieces = rows // LANES
     message = in_ref.shape[0] // (slab_count * pencil_count)
+    order = [int(z) for z in parity_order(z_local)]
 
     def taken(row):
         return in_ref[pl.ds(row, slab_count, stride=pencil_count * message), :]
@@ -311,19 +345,23 @@
         halves.append(jnp.concatenate(parts, axis=1)[:, : rows // 2])
     shared = jnp.concatenate(halves, axis=1)
 
-    def send(piece):
-        here = pl.ds(piece * LANES, LANES)
-        return pltpu.make_async_copy(field_ref.at[here], out_ref.at[here], sent.at[piece])
-
+    def send(place):
+        source = field_ref.at[pl.ds(place * y_local, y_local)]
+        target = out_ref.at[pl.ds(order[place] * y_local, y_local)]
+        return pltpu.make_async_copy(source, target, sent.at[place])
+
+    done = 0
     for piece in range(pieces):
         here = slice(piece * LANES, (piece + 1) * LANES)
         block = [taken(q * message + piece) for q in range(pencil_count)]
         block.append(shared[:, here])
         field = product(split(jnp.concatenate(block, axis=0).T), table, ((1,), (0,)))
         field_ref[here, :] = mean_ref[here, :] + field
-        send(piece).start()
-    for piece in range(pieces):
-        send(piece).wait()
+        while (done + 1) * y_local <= (piece + 1) * LANES:
+            send(done).start()
+            done += 1
+    for place in range(z_local):
+        send(place).wait()
 
 
 def whole():
@@ -358,9 +396,19 @@
     cell_total = float(z_length * y_length * x_length)
     x_order = (np.arange(slab_count)[None, :] * kx_local + np.arange(kx_local)[:, None]).reshape(-1)
     x_table = hartley(x_order, np.arange(x_length), x_length)
-    y_table = hartley(np.arange(y_length), np.arange(y_length), y_length)
-    z_order = (np.arange(slab_count)[None, :] * z_local + np.arange(z_local)[:, None]).reshape(-1)
-    z_table = hartley(z_order, np.arange(z_length), z_length)
+    y_half = np.arange(y_length // 2)
+    y_table = [
+        np.stack(terms)
+        for terms in zip(
+            hartley(2 * y_half, y_half, y_length),
+            hartley(2 * y_half + 1, y_half, y_length),
+            hartley(y_half, 2 * y_half + 1, y_length),
+        )
+    ]
+    z_order = (
+        np.arange(slab_count)[None, :] * z_local + parity_order(z_local)[:, None]
+    ).reshape(-1)
+    z_table = hartley(z_order, np.arange(z_length // 2), z_length)
     place = jnp.stack([lax.axis_index(SLAB), lax.axis_index("pencil")]).astype(jnp.int32)
     place, species = lax.optimization_barrier((place, species))
 
@@ -409,7 +457,10 @@
         mean_kernel,
         grid=(z_local,),
         in_specs=[scalars(), scalars(), whole(), plane_in, whole(), whole()],
-        out_specs=[pl.BlockSpec((1, y_local, x_length), lambda z: (z, 0, 0)), whole()],
+        out_specs=[
+            pl.BlockSpec((1, y_local, x_length), lambda z: (parity_place(z, z_local), 0, 0)),
+            whole(),
+        ],
         out_shape=[
             jax.ShapeDtypeStruct((z_local, y_local, x_length), f32),
             jax.ShapeDtypeStruct((slots, entries), f32),
@@ -439,13 +490,15 @@
     )(place, moved, *z_table, *y_table)
     moved = exchange(packed)
     new_density = pl.pallas_call(
-        functools.partial(x_inverse_kernel, slab_count=slab_count, pencil_count=pencil_count),
+        functools.partial(
+            x_inverse_kernel, slab_count=slab_count, pencil_count=pencil_count, z_local=z_local
+        ),
         in_specs=[whole()] * 4,
         out_specs=pl.BlockSpec(memory_space=pltpu.HBM),
         out_shape=jax.ShapeDtypeStruct((z_local * y_local, x_length), f32),
         scratch_shapes=[
             pltpu.VMEM((z_local * y_local, x_length), f32),
-            pltpu.SemaphoreType.DMA((z_local * y_local // LANES,)),
+            pltpu.SemaphoreType.DMA((z_local,)),
         ],
         compiler_params=params(24),
         name="x_inverse",

time: 120 us -> 119 us (level)
  Pallas kernels: 18.8 us -> 17.4 us
    pallas_call x1, Pallas kernels: 7.16 us -> 5.75 us  [body(): pl.pallas_call(functools.partial(plane_kernel, slab_count=slab_count, pen...]
where the time goes in v2:
time: 119 us; the launch traced here: 118 us
  blocking collectives  64.6 us (54%)
  waiting for transfers between devices  25.2 us (21%)
  Pallas kernels  17.4 us (15%)
  starting transfers between devices  6.63 us (6%)
  local copies, waits for them, and re-layouts  2.99 us (3%)
  between operations  1.45 us (1%)
    all_to_all x2, blocking collectives, exchange(): lax.all_to_all(array.reshape(devices, -1, 1, LANES), SLAB_PENCIL, split_a...  64.6 us
    all_to_all x1, waiting for transfers between devices, exchange(): lax.all_to_all(array.reshape(devices, -1, 1, LANES), SLAB_PENCIL, split_a...  25.2 us
    all_to_all x1, starting transfers between devices, exchange(): lax.all_to_all(array.reshape(devices, -1, 1, LANES), SLAB_PENCIL, split_a...  6.63 us
    pallas_call x1, Pallas kernels, body(): pl.pallas_call(functools.partial(plane_kernel, slab_count=slab_count, pen...  5.75 us
    pallas_call x1, Pallas kernels, body(): pl.pallas_call(functools.partial(gram_kernel, cell_total=cell_total, bloc...  4.56 us
    unnamed x20, local copies, waits for them, and re-layouts  2.99 us
    pallas_call x1, Pallas kernels, body(): pl.pallas_call(mean_kernel, grid=(z_local,), in_specs=[scalars(), scalars...  2.67 us
    pallas_call x1, Pallas kernels, body(): pl.pallas_call(functools.partial(x_inverse_kernel, slab_count=slab_count,...  2.39 us
  transfers between devices with their start and end apart: 1, of which 1 were waited for; matrix products, arithmetic and copies ran while one was open for 0% of the time, Pallas kernels for 2%

profile of v2, /device:TPU:1, one launch (start us, length us, event | category | flops | bytes accessed | tf_op | source)
XLA Modules:
  0.0 118.3 jit_solution(904525415421618549)
XLA Ops:
  0.6 0.0 copy-start.2
  0.6 0.0 copy-start.3
  1.4 0.1 pad_add_fusion.place_ref
  1.4 0.0 copy-start.4
  1.4 0.0 copy-start.5
  1.4 0.0 copy-start.7
  1.4 0.0 copy-start.8
  1.4 4.6 %gram.1 = (f32[256,128]{1,0:T(8,128)S(1)}, f32[7,8,80,320]{3,2,1,0:T(8,128)S(1)}) custom-call(s32[24]{0:T(128)} %species_ref.1, s32[1]{0:T(128)S(6)} %copy.17.count_ref, f32[7,8,80,320]{3,2,1,0:T(8,128)} %residual_ref.1, f32[7,24,324]{2,1,0:T(8,128)} %block_residual_ref.1), custom_call_target="tpu_custom_call" | custom-call | tf_op jit(solution)/shard_map/gram/pallas_call | solution.py:415
  6.0 28.2 %all_to_all.15 = f32[256,1,1,128]{3,2,1,0:T(1,128)S(1)} all-to-all(f32[256,1,1,128]{3,2,1,0:T(1,128)S(1)} %bitcast.21), channel_id=1, replica_groups=mesh['slab_0'=8,'slab_1'=4,'slab_2'=2,'pencil'=4] {'slab_0','slab_1','sl..., dimensions={0} | all-to-all | bytes 262144 | tf_op jit(solution)/shard_map/all_to_all | solution.py:434
  34.3 0.0 copy-done.2
  34.3 0.0 copy-done.3
  34.3 0.0 copy-start.1
  34.3 0.0 copy-start.6
  34.3 0.0 copy-start.9
  34.3 2.0 %mix.1 = (f32[2048,128]{1,0:T(8,128)S(1)}, f32[8,128]{1,0:T(8,128)S(1)}) custom-call(f32[256,128]{1,0:T(8,128)S(1)} %bitcast.20, f32[7,8,80,320]{3,2,1,0:T(8,128)S(1)} %get-tuple-element.13.residual_ref, bf16[320,320]{1,0:T(8,128)(2,1)S(1)} %copy-done.3, bf16[320,320]{1,0:T(8,128)(2,1)S(1)} %copy-done.2), custom_call_target="tpu_custom_call" | custom-call | tf_op jit(solution)/shard_map/mix/pallas_call | solution.py:439
  36.3 36.3 %all_to_all.16 = f32[256,8,1,128]{3,1,2,0:T(8,128)S(1)} all-to-all(f32[256,8,1,128]{3,1,2,0:T(8,128)S(1)} %bitcast.18), channel_id=1, replica_groups=mesh['slab_0'=8,'slab_1'=4,'slab_2'=2,'pencil'=4] {'slab_0','slab_1','sl..., dimensions={0} | all-to-all | bytes 2097152 | tf_op jit(solution)/shard_map/all_to_all | solution.py:434
  72.7 0.0 copy-done.4
  72.7 0.0 copy-done.5
  72.7 0.0 copy-done.7
  72.7 0.0 copy-done.8
  72.7 5.7 %plane.1 = f32[2048,128]{1,0:T(8,128)} custom-call(s32[2]{0:T(128)S(1)} %pad_add_fusion.place_ref, f32[2048,128]{1,0:T(8,128)S(1)} %bitcast.16, bf16[512,256]{1,0:T(8,128)(2,1)S(1)} %copy-done.5, bf16[512,256]{1,0:T(8,128)(2,1)S(1)} %copy-done.4, bf16[3,160,160]{2,1,0:T(8,128)(2,1)S(1)} %copy-done.8, bf16[3,160,160]{2,1,0:T(8,128)(2,1)S(1)} %copy-done.7), custom_call_target="tpu_custom_call" | custom-call | tf_op jit(solution)/shard_map/plane/pallas_call | solution.py:471
  78.4 6.6 %all-to-all-start.2 = ((f32[256,8,1,128]{3,1,2,0:T(8,128)}), f32[256,8,1,128]{3,1,2,0:T(8,128)S(1)}, u32[]{:S(2)}, u32[]{:S(2)}) async-start(f32[256,8,1,128]{3,1,2,0:T(8,128)} %bitcast.9), calls=%async_computation.2 | async-start | bytes 2097152 | tf_op jit(solution)/shard_map/all_to_all | solution.py:434
  85.1 0.0 copy-done.1
  85.1 0.0 copy-done.6
  85.1 0.0 copy-done.9
  85.1 0.0 copy-start
  85.1 2.9 %copy-done = f32[7,8,80,320]{3,2,1,0:T(8,128)S(1)} copy-done((f32[7,8,80,320]{3,2,1,0:T(8,128)S(1)}, f32[7,8,80,320]{3,2,1,0:T(8,128)}, u32[]{:S(2)}) %copy-start) | copy-done | bytes 5734424
  88.1 2.7 %mean.1 = (f32[8,80,320]{2,1,0:T(8,128)S(1)}, f32[24,324]{1,0:T(8,128)}) custom-call(s32[24]{0:T(128)S(1)} %copy-done.9, s32[1]{0:T(128)S(6)} %copy.17.count_ref, f32[8,128]{1,0:T(8,128)S(1)} %get-tuple-element.15.weights_ref, f32[7,8,80,320]{3,2,1,0:T(8,128)S(1)} %copy-done, f32[7,24,324]{2,1,0:T(8,128)S(1)} %copy-done.6, f32[7,24,324]{2,1,0:T(8,128)S(1)} %copy-done.1), custom_call_target="tpu_custom_call" | custom-call | tf_op jit(solution)/shard_map/mean/pallas_call | solution.py:456
  90.7 25.2 %all-to-all-done.2 = f32[256,8,1,128]{3,1,2,0:T(8,128)S(1)} async-done(((f32[256,8,1,128]{3,1,2,0:T(8,128)}), f32[256,8,1,128]{3,1,2,0:T(8,128)S(1)}, u32[]{:S(2)}, u32[]{:S(2)}) %all-to-all-start.2) | async-done | bytes 1048608 | tf_op jit(solution)/shard_map/all_to_all | solution.py:434
  115.9 2.4 %x_inverse.1 = f32[640,320]{1,0:T(8,128)} custom-call(f32[2048,128]{1,0:T(8,128)S(1)} %bitcast.17, f32[640,320]{1,0:T(8,128)S(1)} %bitcast.19, bf16[320,320]{1,0:T(8,128)(2,1)S(1)} %copy-done.3, bf16[320,320]{1,0:T(8,128)(2,1)S(1)} %copy-done.2), custom_call_target="tpu_custom_call" | custom-call | tf_op jit(solution)/shard_map/x_inverse/pallas_call | solution.py:492
Async XLA Ops:
  0.6 33.6 %copy-start.2 = (bf16[320,320]{1,0:T(8,128)(2,1)S(1)}, bf16[320,320]{1,0:T(8,128)(2,1)}, u32[]{:S(2)}) copy-start(bf16[320,320]{1,0:T(8,128)(2,1)} %constant.34.clone.low_ref) | copy-start | bytes 614404
  0.6 33.6 %copy-start.3 = (bf16[320,320]{1,0:T(8,128)(2,1)S(1)}, bf16[320,320]{1,0:T(8,128)(2,1)}, u32[]{:S(2)}) copy-start(bf16[320,320]{1,0:T(8,128)(2,1)} %constant.33.clone.high_ref) | copy-start | bytes 614404
  1.4 71.2 %copy-start.4 = (bf16[512,256]{1,0:T(8,128)(2,1)S(1)}, bf16[512,256]{1,0:T(8,128)(2,1)}, u32[]{:S(2)}) copy-start(bf16[512,256]{1,0:T(8,128)(2,1)} %constant.36.clone.zl_ref) | copy-start | bytes 786436
  1.4 71.2 %copy-start.5 = (bf16[512,256]{1,0:T(8,128)(2,1)S(1)}, bf16[512,256]{1,0:T(8,128)(2,1)}, u32[]{:S(2)}) copy-start(bf16[512,256]{1,0:T(8,128)(2,1)} %constant.35.clone.zh_ref) | copy-start | bytes 786436
  1.4 71.2 %copy-start.7 = (bf16[3,160,160]{2,1,0:T(8,128)(2,1)S(1)}, bf16[3,160,160]{2,1,0:T(8,128)(2,1)}, u32[]{:S(2)}) copy-start(bf16[3,160,160]{2,1,0:T(8,128)(2,1)} %constant.38.clone.yl_ref) | copy-start | bytes 460804
  1.4 71.2 %copy-start.8 = (bf16[3,160,160]{2,1,0:T(8,128)(2,1)S(1)}, bf16[3,160,160]{2,1,0:T(8,128)(2,1)}, u32[]{:S(2)}) copy-start(bf16[3,160,160]{2,1,0:T(8,128)(2,1)} %constant.37.clone.yh_ref) | copy-start | bytes 460804
  34.3 50.8 %copy-start.1 = (f32[7,24,324]{2,1,0:T(8,128)S(1)}, f32[7,24,324]{2,1,0:T(8,128)}, u32[]{:S(2)}) copy-start(f32[7,24,324]{2,1,0:T(8,128)} %block_residual_ref.1) | copy-start | bytes 653188
  34.3 50.8 %copy-start.6 = (f32[7,24,324]{2,1,0:T(8,128)S(1)}, f32[7,24,324]{2,1,0:T(8,128)}, u32[]{:S(2)}) copy-start(f32[7,24,324]{2,1,0:T(8,128)} %block_ref.3) | copy-start | bytes 653188
  34.3 50.8 %copy-start.9 = (s32[24]{0:T(128)S(1)}, s32[24]{0:T(128)}, u32[]{:S(2)}) copy-start(s32[24]{0:T(128)} %species_ref.1) | copy-start | bytes 292
  78.4 37.5 %all-to-all-start.2 = ((f32[256,8,1,128]{3,1,2,0:T(8,128)}), f32[256,8,1,128]{3,1,2,0:T(8,128)S(1)}, u32[]{:S(2)}, u32[]{:S(2)}) async-start(f32[256,8,1,128]{3,1,2,0:T(8,128)} %bitcast.9), calls=%async_computation.2 | async-start | bytes 2097152 | tf_op jit(solution)/shard_map/all_to_all | solution.py:434
  85.1 3.0 %copy-start = (f32[7,8,80,320]{3,2,1,0:T(8,128)S(1)}, f32[7,8,80,320]{3,2,1,0:T(8,128)}, u32[]{:S(2)}) copy-start(f32[7,8,80,320]{3,2,1,0:T(8,128)} %density_ref.1) | copy-start | bytes 17203204

commit v3 on v1

--- a/solution.py
+++ b/solution.py
@@ -23,6 +23,7 @@
 bf16 = jnp.bfloat16
 LANES = 128
 MIB = 1 << 20
+FETCH_AHEAD = 4
 
 
 def pair_list(histories):
@@ -84,7 +85,8 @@
     def fetch(z):
         return pltpu.make_async_copy(residual_ref.at[:, z], held_ref.at[:, z], arrived.at[z])
 
-    for z in range(planes):
+    ahead = min(FETCH_AHEAD, planes)
+    for z in range(ahead):
         fetch(z).start()
     acc_ref[...] = jnp.zeros_like(acc_ref)
     _, slots, entries = block_ref.shape
@@ -97,6 +99,10 @@
         line = jnp.where(lane == k, block_part, line)
 
     def plane(z, carry):
+        @pl.when(z + ahead < planes)
+        def _():
+            fetch(z + ahead).start()
+
         fetch(z).wait()
         for start in range(0, width, LANES):
             lanes = slice(start, min(start + LANES, width))
@@ -158,27 +164,28 @@
         for i in range(1, histories):
             mixed = mixed + weights[i] * residual_ref[i, z]
         high, low = split(mixed)
-        mixed_high[z * rows : (z + 1) * rows, :] = high
-        mixed_low[z * rows : (z + 1) * rows, :] = low
+        filler = jnp.zeros((LANES - rows, mixed.shape[1]), bf16)
+        mixed_high[z * LANES : z * LANES + rows, :] = high
+        mixed_high[z * LANES + rows : (z + 1) * LANES, :] = filler
+        mixed_low[z * LANES : z * LANES + rows, :] = low
+        mixed_low[z * LANES + rows : (z + 1) * LANES, :] = filler
     table = (high_ref[...], low_ref[...])
     result = product(table, (mixed_high[...], mixed_low[...]), ((1,), (1,)))
-    pieces = result.shape[1] // LANES
     own_planes = result.shape[0] // slab_count - 1
-    message = out_ref.shape[0] // (slab_count * own_planes)
-    period = own_planes * message
-    extra = message - pieces
-
-    def put(row, plane, piece):
-        out_ref[pl.ds(row, slab_count, stride=period), :] = result[
-            plane * slab_count : (plane + 1) * slab_count, piece * LANES : (piece + 1) * LANES
+    period = own_planes * planes
+    part = rows // 2
+    lane = lax.broadcasted_iota(jnp.int32, (slab_count, LANES), 1)
+    here = (lane >= rows) & (lane < rows + part)
+    for z in range(planes):
+        columns = slice(z * LANES, (z + 1) * LANES)
+        shared = result[own_planes * slab_count :, columns]
+        shared = [
+            jnp.where(here, pltpu.roll(shared, shift, 1), 0.0) for shift in (rows, rows - part)
         ]
-
-    for own in range(own_planes):
-        for piece in range(pieces):
-            put(own * message + piece, own, piece)
-        first = (pieces - extra) * (own // 2)
-        for piece in range(extra):
-            put(own * message + pieces + piece, own_planes, first + piece)
+        for own in range(own_planes):
+            out_ref[pl.ds(own * planes + z, slab_count, stride=period), :] = (
+                result[own * slab_count : (own + 1) * slab_count, columns] + shared[own // 2]
+            )
 
 
 def plane_kernel(
@@ -189,85 +196,71 @@
     yh_ref,
     yl_ref,
     out_ref,
-    main_ref,
-    half_ref,
     *,
-    slab_count,
-    pencil_count,
-    z_local,
-    y_local,
     x_length,
+    y_length,
+    z_length,
     scale,
 ):
-    z_length = slab_count * z_local
-    y_length = pencil_count * y_local
-    message = in_ref.shape[0] // (slab_count * pencil_count)
-    period = pencil_count * message
-    pieces = z_local * y_local // LANES
-    extra = message - pieces
-    half = z_local // 2
-    half_rows = half * y_local
-    spare = pieces * LANES - half_rows - (pieces - extra) * LANES
+    slab_count, pencil_count, z_local, _ = in_ref.shape
+    z_half = z_length // 2
+    y_half = y_length // 2
+    s_half = slab_count // 2
+    fold = pencil_count // 2 * LANES
     in_half = place_ref[1] // 2
     out_half = place_ref[1] % 2
 
-    def taken(row):
-        return in_ref[pl.ds(row, slab_count, stride=period), :].T
-
-    def spread(rows, count):
-        return jnp.concatenate([rows[z * y_local : (z + 1) * y_local] for z in range(count)], axis=1)
-
-    def stacked(block, count):
+    def gathered(first):
         return jnp.concatenate(
-            [block[:, z * slab_count : (z + 1) * slab_count] for z in range(count)], axis=0
+            [
+                in_ref[first : first + s_half, q].reshape(z_half, LANES)
+                for q in range(pencil_count)
+            ],
+            axis=1,
         )
 
-    for q in range(pencil_count):
-        here = slice(q * y_local, (q + 1) * y_local)
-        rows = jnp.concatenate([taken(q * message + k) for k in range(pieces)], axis=0)
-        main_ref[here, :] = spread(rows, z_local)
-        rows = jnp.concatenate([taken(q * message + pieces + k) for k in range(extra)], axis=0)
-        rows = jnp.where(in_half == 0, rows[:half_rows], rows[spare : spare + half_rows])
-        half_ref[here, :] = spread(rows, half)
-
-    z_table = (zh_ref[...], zl_ref[...])
-    y_table = (yh_ref[...], yl_ref[...])
-
-    def half_table(which):
-        rows = pl.ds(pl.multiple_of(which * (z_length // 2), LANES), z_length // 2)
-        return (zh_ref[rows, :], zl_ref[rows, :])
-
+    def z_table(kind):
+        return (zh_ref[kind], zl_ref[kind])
+
+    def y_table(half, kind):
+        return (yh_ref[2 * half + kind], yl_ref[2 * half + kind])
+
+    low, high = gathered(0), gathered(s_half)
     lines = jnp.concatenate(
         [
-            product(split(main_ref[...]), z_table, ((1,), (0,))),
-            product(split(half_ref[...]), half_table(in_half), ((1,), (0,))),
-        ],
-        axis=1,
+            product(z_table(0), split(low + high), ((1,), (0,))),
+            product(z_table(1), split(low - high), ((1,), (0,))),
+        ],
+        axis=0,
     )
-    spectrum = product(y_table, split(lines), ((1,), (0,)))
-    freq_y = lax.broadcasted_iota(jnp.int32, (y_length, z_length), 0)
-    freq_z = lax.broadcasted_iota(jnp.int32, (y_length, z_length), 1)
-    mag_y = jnp.minimum(freq_y, y_length - freq_y).astype(f32)
-    mag_z = jnp.minimum(freq_z, z_length - freq_z).astype(f32)
-    plane = mag_y * mag_y + mag_z * mag_z
-    kept = []
-    for j, own in enumerate((place_ref[1], pencil_count)):
-        freq_x = place_ref[0] * (pencil_count + 1) + own
-        mag_x = jnp.minimum(freq_x, x_length - freq_x).astype(f32)
-        square = plane + mag_x * mag_x
-        factor = square / (square + kerker_wave * kerker_wave) * scale
-        kept.append(spectrum[:, j * z_length : (j + 1) * z_length] * factor)
-    kept = product(y_table, split(jnp.concatenate(kept, axis=1)), ((1,), (0,)))
-    main = product(split(kept[:, :z_length]), z_table, ((1,), (1,)))
-    part = product(split(kept[:, z_length:]), half_table(out_half), ((1,), (1,)))
-    filler = jnp.zeros((extra * LANES - half_rows, slab_count), f32)
+    folded = [lines[:, :fold] + lines[:, fold:], lines[:, :fold] - lines[:, fold:]]
+    row = lax.broadcasted_iota(jnp.int32, (z_length, 1), 0)
+    lane = lax.broadcasted_iota(jnp.int32, (1, y_length), 1)
+    freq_z = jnp.where(row < z_half, 2 * row, 2 * row - (z_length - 1))
+    first_x = place_ref[0] * (pencil_count + 1)
+    freq_x = jnp.where(lane < y_half, first_x + place_ref[1], first_x + pencil_count)
+
+    def squared(index, length):
+        least = jnp.minimum(index, length - index).astype(f32)
+        return least * least
+
+    results = []
+    for kind in range(2):
+        spectrum = product(split(folded[kind]), y_table(in_half, kind), ((1,), (0,)))
+        freq_y = 2 * jnp.where(lane < y_half, lane, lane - y_half) + kind
+        square = squared(freq_z, z_length) + (
+            squared(freq_y, y_length) + squared(freq_x, x_length)
+        )
+        kept = spectrum * (square / (square + kerker_wave * kerker_wave) * scale)
+        results.append(product(split(kept), y_table(out_half, kind), ((1,), (1,))))
+    lines = jnp.concatenate([results[0] + results[1], results[0] - results[1]], axis=1)
+    even = product(z_table(0), split(lines[:z_half]), ((1,), (0,)))
+    odd = product(z_table(1), split(lines[z_half:]), ((0,), (0,)))
+    low, high = even + odd, even - odd
     for q in range(pencil_count):
-        here = slice(q * y_local, (q + 1) * y_local)
-        rows = jnp.concatenate([stacked(main[here], z_local), stacked(part[here], half), filler], axis=0)
-        for k in range(message):
-            out_ref[pl.ds(q * message + k, slab_count, stride=period), :] = rows[
-                k * LANES : (k + 1) * LANES
-            ].T
+        columns = slice(q * LANES, (q + 1) * LANES)
+        out_ref[:s_half, q] = low[:, columns].reshape(s_half, z_local, LANES)
+        out_ref[s_half:, q] = high[:, columns].reshape(s_half, z_local, LANES)
 
 
 def mean_kernel(
@@ -292,38 +285,48 @@
 
 
 def x_inverse_kernel(
-    in_ref, mean_ref, high_ref, low_ref, out_ref, field_ref, sent, *, slab_count, pencil_count
+    in_ref,
+    mean_ref,
+    high_ref,
+    low_ref,
+    out_ref,
+    field_ref,
+    sent,
+    *,
+    slab_count,
+    pencil_count,
+    z_local,
 ):
     rows, x_length = mean_ref.shape
+    y_local = rows // z_local
+    part = y_local // 2
     table = (high_ref[...], low_ref[...])
-    pieces = rows // LANES
-    message = in_ref.shape[0] // (slab_count * pencil_count)
-
-    def taken(row):
-        return in_ref[pl.ds(row, slab_count, stride=pencil_count * message), :]
-
-    halves = []
-    for out_half in range(2):
-        parts = [
-            taken(out_half * message + k) + taken((out_half + 2) * message + k)
-            for k in range(pieces, message)
-        ]
-        halves.append(jnp.concatenate(parts, axis=1)[:, : rows // 2])
-    shared = jnp.concatenate(halves, axis=1)
-
-    def send(piece):
-        here = pl.ds(piece * LANES, LANES)
-        return pltpu.make_async_copy(field_ref.at[here], out_ref.at[here], sent.at[piece])
-
-    for piece in range(pieces):
-        here = slice(piece * LANES, (piece + 1) * LANES)
-        block = [taken(q * message + piece) for q in range(pencil_count)]
-        block.append(shared[:, here])
-        field = product(split(jnp.concatenate(block, axis=0).T), table, ((1,), (0,)))
+    lane = lax.broadcasted_iota(jnp.int32, (slab_count, LANES), 1)
+    groups = sent.shape[0]
+    group = z_local // groups
+
+    def send(index):
+        here = pl.ds(index * group * y_local, group * y_local)
+        return pltpu.make_async_copy(field_ref.at[here], out_ref.at[here], sent.at[index])
+
+    for index in range(groups):
+        lines = []
+        for z in range(index * group, (index + 1) * group):
+            block = [
+                in_ref[pl.ds(q * z_local + z, slab_count, stride=pencil_count * z_local), :]
+                for q in range(pencil_count)
+            ]
+            first = pltpu.roll(block[0] + block[2], LANES - y_local, 1)
+            second = pltpu.roll(block[1] + block[3], LANES - y_local + part, 1)
+            block.append(jnp.where(lane < part, first, second))
+            lines.append(jnp.concatenate(block, axis=0).T[:y_local])
+        lines = jnp.concatenate(lines, axis=0)
+        field = product(split(lines), table, ((1,), (0,)))
+        here = slice(index * group * y_local, (index + 1) * group * y_local)
         field_ref[here, :] = mean_ref[here, :] + field
-        send(piece).start()
-    for piece in range(pieces):
-        send(piece).wait()
+        send(index).start()
+    for index in range(groups):
+        send(index).wait()
 
 
 def whole():
@@ -353,14 +356,33 @@
     z_length = z_local * slab_count
     slots, entries = occupancy_residual.shape[1:]
     kx_local = x_length // slab_count
-    message = z_local * y_local // LANES + -(-z_local * y_local // (2 * LANES))
-    rows = devices * message
+    rows = devices * z_local
+    part = y_local // 2
     cell_total = float(z_length * y_length * x_length)
     x_order = (np.arange(slab_count)[None, :] * kx_local + np.arange(kx_local)[:, None]).reshape(-1)
     x_table = hartley(x_order, np.arange(x_length), x_length)
-    y_table = hartley(np.arange(y_length), np.arange(y_length), y_length)
-    z_order = (np.arange(slab_count)[None, :] * z_local + np.arange(z_local)[:, None]).reshape(-1)
-    z_table = hartley(z_order, np.arange(z_length), z_length)
+    y_tables = []
+    for half in range(2):
+        for kind in range(2):
+            freq = 2 * np.arange(y_length // 2) + kind
+            terms = [np.zeros((pencil_count // 2, LANES, 2, y_length // 2), bf16) for _ in range(2)]
+            for q in range(pencil_count // 2):
+                point = q * y_local + np.arange(y_local)
+                whole_terms = hartley(point, freq, y_length)
+                part_terms = hartley(point[half * part : (half + 1) * part], freq, y_length)
+                for term, own, some in zip(terms, whole_terms, part_terms):
+                    term[q, :y_local, 0] = own
+                    term[q, y_local : y_local + part, 1] = some
+            y_tables.append([term.reshape(-1, y_length) for term in terms])
+    y_table = [np.stack(terms) for terms in zip(*y_tables)]
+    z_half = np.arange(z_length // 2)
+    z_table = [
+        np.stack(terms)
+        for terms in zip(
+            hartley(2 * z_half, z_half, z_length),
+            hartley(2 * z_half + 1, z_half, z_length),
+        )
+    ]
     place = jnp.stack([lax.axis_index(SLAB), lax.axis_index("pencil")]).astype(jnp.int32)
     place, species = lax.optimization_barrier((place, species))
 
@@ -384,10 +406,10 @@
 
     def exchange(array):
         return lax.all_to_all(
-            array.reshape(devices, -1, 1, LANES), SLAB_PENCIL, split_axis=0, concat_axis=0, tiled=True
-        ).reshape(-1, LANES)
-
-    sums = exchange(sums)
+            array.reshape(devices, -1, LANES), SLAB_PENCIL, split_axis=0, concat_axis=0, tiled=True
+        )
+
+    sums = exchange(sums).reshape(devices, LANES)
     packed, weights = pl.pallas_call(
         functools.partial(mix_kernel, slab_count=slab_count),
         in_specs=[whole()] * 4,
@@ -397,19 +419,22 @@
             jax.ShapeDtypeStruct((8, LANES), f32),
         ],
         scratch_shapes=[
-            pltpu.VMEM((z_local * y_local, x_length), bf16),
-            pltpu.VMEM((z_local * y_local, x_length), bf16),
+            pltpu.VMEM((z_local * LANES, x_length), bf16),
+            pltpu.VMEM((z_local * LANES, x_length), bf16),
         ],
         compiler_params=params(24),
         name="mix",
     )(sums, held, *x_table)
-    moved = exchange(packed)
+    moved = exchange(packed).reshape(slab_count, pencil_count, z_local, LANES)
     plane_in = pl.BlockSpec((histories, 1, y_local, x_length), lambda z: (0, z, 0, 0))
     mean, new_occupancy = pl.pallas_call(
         mean_kernel,
         grid=(z_local,),
         in_specs=[scalars(), scalars(), whole(), plane_in, whole(), whole()],
-        out_specs=[pl.BlockSpec((1, y_local, x_length), lambda z: (z, 0, 0)), whole()],
+        out_specs=[
+            pl.BlockSpec((1, y_local, x_length), lambda z: (z, 0, 0)),
+            whole(),
+        ],
         out_shape=[
             jax.ShapeDtypeStruct((z_local, y_local, x_length), f32),
             jax.ShapeDtypeStruct((slots, entries), f32),
@@ -420,32 +445,28 @@
     packed = pl.pallas_call(
         functools.partial(
             plane_kernel,
-            slab_count=slab_count,
-            pencil_count=pencil_count,
-            z_local=z_local,
-            y_local=y_local,
             x_length=x_length,
+            y_length=y_length,
+            z_length=z_length,
             scale=grid_mixing / cell_total,
         ),
         in_specs=[scalars()] + [whole()] * 5,
         out_specs=whole(),
-        out_shape=jax.ShapeDtypeStruct((rows, LANES), f32),
-        scratch_shapes=[
-            pltpu.VMEM((y_length, z_length), f32),
-            pltpu.VMEM((y_length, z_length // 2), f32),
-        ],
+        out_shape=jax.ShapeDtypeStruct((slab_count, pencil_count, z_local, LANES), f32),
         compiler_params=params(32),
         name="plane",
     )(place, moved, *z_table, *y_table)
-    moved = exchange(packed)
+    moved = exchange(packed).reshape(rows, LANES)
     new_density = pl.pallas_call(
-        functools.partial(x_inverse_kernel, slab_count=slab_count, pencil_count=pencil_count),
+        functools.partial(
+            x_inverse_kernel, slab_count=slab_count, pencil_count=pencil_count, z_local=z_local
+        ),
         in_specs=[whole()] * 4,
         out_specs=pl.BlockSpec(memory_space=pltpu.HBM),
         out_shape=jax.ShapeDtypeStruct((z_local * y_local, x_length), f32),
         scratch_shapes=[
             pltpu.VMEM((z_local * y_local, x_length), f32),
-            pltpu.SemaphoreType.DMA((z_local * y_local // LANES,)),
+            pltpu.SemaphoreType.DMA((2,)),
         ],
         compiler_params=params(24),
         name="x_inverse",

time: 120 us -> 119 us (level)
    pallas_call x1, Pallas kernels: 7.16 us -> 5.15 us  [body(): pl.pallas_call(functools.partial(plane_kernel, x_length=x_length, y_lengt...]
where the time goes in v3:
time: 119 us
  blocking collectives  64.6 us (54%)
  waiting for transfers between devices  25.2 us (21%)
  Pallas kernels  17.6 us (15%)
  starting transfers between devices  6.62 us (6%)
  local copies, waits for them, and re-layouts  2.99 us (3%)
  between operations  1.45 us (1%)
    all_to_all x2, blocking collectives, exchange(): lax.all_to_all(array.reshape(devices, -1, LANES), SLAB_PENCIL, split_axis...  64.6 us
    all_to_all x1, waiting for transfers between devices, exchange(): lax.all_to_all(array.reshape(devices, -1, LANES), SLAB_PENCIL, split_axis...  25.2 us
    all_to_all x1, starting transfers between devices, exchange(): lax.all_to_all(array.reshape(devices, -1, LANES), SLAB_PENCIL, split_axis...  6.62 us
    pallas_call x1, Pallas kernels, body(): pl.pallas_call(functools.partial(plane_kernel, x_length=x_length, y_lengt...  5.15 us
    pallas_call x1, Pallas kernels, body(): pl.pallas_call(functools.partial(gram_kernel, cell_total=cell_total, bloc...  4.9 us
    unnamed x20, local copies, waits for them, and re-layouts  2.99 us
    pallas_call x1, Pallas kernels, body(): pl.pallas_call(mean_kernel, grid=(z_local,), in_specs=[scalars(), scalars...  2.67 us
    pallas_call x1, Pallas kernels, body(): pl.pallas_call(functools.partial(x_inverse_kernel, slab_count=slab_count,...  2.58 us
  transfers between devices with their start and end apart: 1, of which 1 were waited for; matrix products, arithmetic and copies ran while one was open for 0% of the time, Pallas kernels for 2%

profile of v3, /device:TPU:1, one launch (start us, length us, event | category | flops | bytes accessed | tf_op | source)
XLA Modules:
  0.0 118.6 jit_solution(18039371649464466726)
XLA Ops:
  0.6 0.0 copy-start.2
  0.6 0.0 copy-start.3
  1.4 0.1 pad_add_fusion.place_ref
  1.4 0.0 copy-start.4
  1.4 0.0 copy-start.5
  1.4 0.0 copy-start.6
  1.4 0.0 copy-start.7
  1.4 4.9 %gram.1 = (f32[256,128]{1,0:T(8,128)S(1)}, f32[7,8,80,320]{3,2,1,0:T(8,128)S(1)}) custom-call(s32[24]{0:T(128)} %species_ref.1, s32[1]{0:T(128)S(6)} %copy.15.count_ref, f32[7,8,80,320]{3,2,1,0:T(8,128)} %residual_ref.1, f32[7,24,324]{2,1,0:T(8,128)} %block_residual_ref.1), custom_call_target="tpu_custom_call" | custom-call | tf_op jit(solution)/shard_map/gram/pallas_call | solution.py:389
  6.4 28.2 %all_to_all.15 = f32[256,1,128]{2,1,0:T(1,128)S(1)} all-to-all(f32[256,1,128]{2,1,0:T(1,128)S(1)} %bitcast.17), channel_id=1, replica_groups=mesh['slab_0'=8,'slab_1'=4,'slab_2'=2,'pencil'=4] {'slab_0','slab_1','sl..., dimensions={0} | all-to-all | bytes 262144 | tf_op jit(solution)/shard_map/all_to_all | solution.py:408
  34.6 0.0 copy-done.2
  34.6 0.0 copy-done.3
  34.6 0.0 copy-start.1
  34.6 0.0 copy-start.8
  34.6 0.0 copy-start.9
  34.6 2.3 %mix.1 = (f32[2048,128]{1,0:T(8,128)S(1)}, f32[8,128]{1,0:T(8,128)S(1)}) custom-call(f32[256,128]{1,0:T(8,128)S(1)} %bitcast.16, f32[7,8,80,320]{3,2,1,0:T(8,128)S(1)} %get-tuple-element.13.residual_ref, bf16[320,320]{1,0:T(8,128)(2,1)S(1)} %copy-done.3, bf16[320,320]{1,0:T(8,128)(2,1)S(1)} %copy-done.2), custom_call_target="tpu_custom_call" | custom-call | tf_op jit(solution)/shard_map/mix/pallas_call | solution.py:413
  37.0 36.3 %all_to_all.16 = f32[256,8,128]{2,1,0:T(8,128)S(1)} all-to-all(f32[256,8,128]{2,1,0:T(8,128)S(1)} %bitcast.14), channel_id=1, replica_groups=mesh['slab_0'=8,'slab_1'=4,'slab_2'=2,'pencil'=4] {'slab_0','slab_1','sl..., dimensions={0} | all-to-all | bytes 2097152 | tf_op jit(solution)/shard_map/all_to_all | solution.py:408
  73.3 0.0 copy-done.4
  73.3 0.0 copy-done.5
  73.3 0.0 copy-done.6
  73.3 0.0 copy-done.7
  73.3 5.1 %plane.1 = f32[64,4,8,128]{3,2,1,0:T(8,128)} custom-call(s32[2]{0:T(128)S(1)} %pad_add_fusion.place_ref, f32[64,4,8,128]{3,2,1,0:T(8,128)S(1)} %bitcast.12, bf16[2,256,256]{2,1,0:T(8,128)(2,1)S(1)} %copy-done.7, bf16[2,256,256]{2,1,0:T(8,128)(2,1)S(1)} %copy-done.6, bf16[4,256,320]{2,1,0:T(8,128)(2,1)S(1)} %copy-done.5, bf16[4,256,320]{2,1,0:T(8,128)(2,1)S(1)} %copy-done.4), custom_call_target="tpu_custom_call" | custom-call | tf_op jit(solution)/shard_map/plane/pallas_call | solution.py:445
  78.5 6.6 %all-to-all-start.2 = ((f32[256,8,128]{2,1,0:T(8,128)}), f32[256,8,128]{2,1,0:T(8,128)S(1)}, u32[]{:S(2)}, u32[]{:S(2)}) async-start(f32[256,8,128]{2,1,0:T(8,128)} %bitcast.7), calls=%async_computation.2 | async-start | bytes 2097152 | tf_op jit(solution)/shard_map/all_to_all | solution.py:408
  85.1 0.0 copy-done.1
  85.1 0.0 copy-done.8
  85.1 0.0 copy-done.9
  85.1 0.0 copy-start
  85.2 2.9 %copy-done = f32[7,8,80,320]{3,2,1,0:T(8,128)S(1)} copy-done((f32[7,8,80,320]{3,2,1,0:T(8,128)S(1)}, f32[7,8,80,320]{3,2,1,0:T(8,128)}, u32[]{:S(2)}) %copy-start) | copy-done | bytes 5734424
  88.1 2.7 %mean.1 = (f32[8,80,320]{2,1,0:T(8,128)S(1)}, f32[24,324]{1,0:T(8,128)}) custom-call(s32[24]{0:T(128)S(1)} %copy-done.9, s32[1]{0:T(128)S(6)} %copy.15.count_ref, f32[8,128]{1,0:T(8,128)S(1)} %get-tuple-element.15.weights_ref, f32[7,8,80,320]{3,2,1,0:T(8,128)S(1)} %copy-done, f32[7,24,324]{2,1,0:T(8,128)S(1)} %copy-done.8, f32[7,24,324]{2,1,0:T(8,128)S(1)} %copy-done.1), custom_call_target="tpu_custom_call" | custom-call | tf_op jit(solution)/shard_map/mean/pallas_call | solution.py:430
  90.8 25.2 %all-to-all-done.2 = f32[256,8,128]{2,1,0:T(8,128)S(1)} async-done(((f32[256,8,128]{2,1,0:T(8,128)}), f32[256,8,128]{2,1,0:T(8,128)S(1)}, u32[]{:S(2)}, u32[]{:S(2)}) %all-to-all-start.2) | async-done | bytes 1048608 | tf_op jit(solution)/shard_map/all_to_all | solution.py:408
  116.0 2.6 %x_inverse.1 = f32[640,320]{1,0:T(8,128)} custom-call(f32[2048,128]{1,0:T(8,128)S(1)} %bitcast.13, f32[640,320]{1,0:T(8,128)S(1)} %bitcast.15, bf16[320,320]{1,0:T(8,128)(2,1)S(1)} %copy-done.3, bf16[320,320]{1,0:T(8,128)(2,1)S(1)} %copy-done.2), custom_call_target="tpu_custom_call" | custom-call | tf_op jit(solution)/shard_map/x_inverse/pallas_call | solution.py:460
Async XLA Ops:
  0.6 34.0 %copy-start.2 = (bf16[320,320]{1,0:T(8,128)(2,1)S(1)}, bf16[320,320]{1,0:T(8,128)(2,1)}, u32[]{:S(2)}) copy-start(bf16[320,320]{1,0:T(8,128)(2,1)} %constant.34.clone.low_ref) | copy-start | bytes 614404
  0.6 34.0 %copy-start.3 = (bf16[320,320]{1,0:T(8,128)(2,1)S(1)}, bf16[320,320]{1,0:T(8,128)(2,1)}, u32[]{:S(2)}) copy-start(bf16[320,320]{1,0:T(8,128)(2,1)} %constant.33.clone.high_ref) | copy-start | bytes 614404
  1.4 71.9 %copy-start.4 = (bf16[4,256,320]{2,1,0:T(8,128)(2,1)S(1)}, bf16[4,256,320]{2,1,0:T(8,128)(2,1)}, u32[]{:S(2)}) copy-start(bf16[4,256,320]{2,1,0:T(8,128)(2,1)} %constant.38.clone.yl_ref) | copy-start | bytes 1966084
  1.4 71.9 %copy-start.5 = (bf16[4,256,320]{2,1,0:T(8,128)(2,1)S(1)}, bf16[4,256,320]{2,1,0:T(8,128)(2,1)}, u32[]{:S(2)}) copy-start(bf16[4,256,320]{2,1,0:T(8,128)(2,1)} %constant.37.clone.yh_ref) | copy-start | bytes 1966084
  1.4 71.9 %copy-start.6 = (bf16[2,256,256]{2,1,0:T(8,128)(2,1)S(1)}, bf16[2,256,256]{2,1,0:T(8,128)(2,1)}, u32[]{:S(2)}) copy-start(bf16[2,256,256]{2,1,0:T(8,128)(2,1)} %constant.36.clone.zl_ref) | copy-start | bytes 786436
  1.4 71.9 %copy-start.7 = (bf16[2,256,256]{2,1,0:T(8,128)(2,1)S(1)}, bf16[2,256,256]{2,1,0:T(8,128)(2,1)}, u32[]{:S(2)}) copy-start(bf16[2,256,256]{2,1,0:T(8,128)(2,1)} %constant.35.clone.zh_ref) | copy-start | bytes 786436
  34.6 50.5 %copy-start.1 = (f32[7,24,324]{2,1,0:T(8,128)S(1)}, f32[7,24,324]{2,1,0:T(8,128)}, u32[]{:S(2)}) copy-start(f32[7,24,324]{2,1,0:T(8,128)} %block_residual_ref.1) | copy-start | bytes 653188
  34.6 50.5 %copy-start.8 = (f32[7,24,324]{2,1,0:T(8,128)S(1)}, f32[7,24,324]{2,1,0:T(8,128)}, u32[]{:S(2)}) copy-start(f32[7,24,324]{2,1,0:T(8,128)} %block_ref.3) | copy-start | bytes 653188
  34.6 50.5 %copy-start.9 = (s32[24]{0:T(128)S(1)}, s32[24]{0:T(128)}, u32[]{:S(2)}) copy-start(s32[24]{0:T(128)} %species_ref.1) | copy-start | bytes 292
  78.5 37.5 %all-to-all-start.2 = ((f32[256,8,128]{2,1,0:T(8,128)}), f32[256,8,128]{2,1,0:T(8,128)S(1)}, u32[]{:S(2)}, u32[]{:S(2)}) async-start(f32[256,8,128]{2,1,0:T(8,128)} %bitcast.7), calls=%async_computation.2 | async-start | bytes 2097152 | tf_op jit(solution)/shard_map/all_to_all | solution.py:408
  85.1 3.0 %copy-start = (f32[7,8,80,320]{3,2,1,0:T(8,128)S(1)}, f32[7,8,80,320]{3,2,1,0:T(8,128)}, u32[]{:S(2)}) copy-start(f32[7,8,80,320]{3,2,1,0:T(8,128)} %density_ref.1) | copy-start | bytes 17203204

commit v4 on v3

--- a/solution.py
+++ b/solution.py
@@ -23,7 +23,6 @@
 bf16 = jnp.bfloat16
 LANES = 128
 MIB = 1 << 20
-FETCH_AHEAD = 4
 
 
 def pair_list(histories):
@@ -85,8 +84,7 @@
     def fetch(z):
         return pltpu.make_async_copy(residual_ref.at[:, z], held_ref.at[:, z], arrived.at[z])
 
-    ahead = min(FETCH_AHEAD, planes)
-    for z in range(ahead):
+    for z in range(planes):
         fetch(z).start()
     acc_ref[...] = jnp.zeros_like(acc_ref)
     _, slots, entries = block_ref.shape
@@ -99,10 +97,6 @@
         line = jnp.where(lane == k, block_part, line)
 
     def plane(z, carry):
-        @pl.when(z + ahead < planes)
-        def _():
-            fetch(z + ahead).start()
-
         fetch(z).wait()
         for start in range(0, width, LANES):
             lanes = slice(start, min(start + LANES, width))
@@ -172,20 +166,30 @@
     table = (high_ref[...], low_ref[...])
     result = product(table, (mixed_high[...], mixed_low[...]), ((1,), (1,)))
     own_planes = result.shape[0] // slab_count - 1
-    period = own_planes * planes
     part = rows // 2
     lane = lax.broadcasted_iota(jnp.int32, (slab_count, LANES), 1)
     here = (lane >= rows) & (lane < rows + part)
-    for z in range(planes):
-        columns = slice(z * LANES, (z + 1) * LANES)
-        shared = result[own_planes * slab_count :, columns]
-        shared = [
-            jnp.where(here, pltpu.roll(shared, shift, 1), 0.0) for shift in (rows, rows - part)
+    shared = []
+    for shift in (rows, rows - part):
+        shared.append(
+            [
+                jnp.where(
+                    here,
+                    pltpu.roll(
+                        result[own_planes * slab_count :, z * LANES : (z + 1) * LANES], shift, 1
+                    ),
+                    0.0,
+                )
+                for z in range(planes)
+            ]
+        )
+    for own in range(own_planes):
+        lines = [
+            result[own * slab_count : (own + 1) * slab_count, z * LANES : (z + 1) * LANES]
+            + shared[own // 2][z]
+            for z in range(planes)
         ]
-        for own in range(own_planes):
-            out_ref[pl.ds(own * planes + z, slab_count, stride=period), :] = (
-                result[own * slab_count : (own + 1) * slab_count, columns] + shared[own // 2]
-            )
+        out_ref[:, own] = jnp.swapaxes(jnp.stack(lines), 0, 1)
 
 
 def plane_kernel(
@@ -196,6 +200,8 @@
     yh_ref,
     yl_ref,
     out_ref,
+    made_ref,
+    sent,
     *,
     x_length,
     y_length,
@@ -254,13 +260,28 @@
         kept = spectrum * (square / (square + kerker_wave * kerker_wave) * scale)
         results.append(product(split(kept), y_table(out_half, kind), ((1,), (1,))))
     lines = jnp.concatenate([results[0] + results[1], results[0] - results[1]], axis=1)
-    even = product(z_table(0), split(lines[:z_half]), ((1,), (0,)))
-    odd = product(z_table(1), split(lines[z_half:]), ((0,), (0,)))
-    low, high = even + odd, even - odd
+    sends = []
     for q in range(pencil_count):
-        columns = slice(q * LANES, (q + 1) * LANES)
-        out_ref[:s_half, q] = low[:, columns].reshape(s_half, z_local, LANES)
-        out_ref[s_half:, q] = high[:, columns].reshape(s_half, z_local, LANES)
+        for first in (0, s_half):
+            here = pl.ds(first, s_half)
+            sends.append(
+                pltpu.make_async_copy(
+                    made_ref.at[here, q], out_ref.at[here, q], sent.at[len(sends)]
+                )
+            )
+    for start in range(0, pencil_count, 2):
+        columns = slice(start * LANES, (start + 2) * LANES)
+        even = product(z_table(0), split(lines[:z_half, columns]), ((1,), (0,)))
+        odd = product(z_table(1), split(lines[z_half:, columns]), ((0,), (0,)))
+        low, high = even + odd, even - odd
+        for q in (start, start + 1):
+            columns = slice((q - start) * LANES, (q - start + 1) * LANES)
+            made_ref[:s_half, q] = low[:, columns].reshape(s_half, z_local, LANES)
+            sends[2 * q].start()
+            made_ref[s_half:, q] = high[:, columns].reshape(s_half, z_local, LANES)
+            sends[2 * q + 1].start()
+    for send in sends:
+        send.wait()
 
 
 def mean_kernel(
@@ -309,13 +330,11 @@
         here = pl.ds(index * group * y_local, group * y_local)
         return pltpu.make_async_copy(field_ref.at[here], out_ref.at[here], sent.at[index])
 
+    blocks = [jnp.swapaxes(in_ref[:, q], 0, 1) for q in range(pencil_count)]
     for index in range(groups):
         lines = []
         for z in range(index * group, (index + 1) * group):
-            block = [
-                in_ref[pl.ds(q * z_local + z, slab_count, stride=pencil_count * z_local), :]
-                for q in range(pencil_count)
-            ]
+            block = [turned[z] for turned in blocks]
             first = pltpu.roll(block[0] + block[2], LANES - y_local, 1)
             second = pltpu.roll(block[1] + block[3], LANES - y_local + part, 1)
             block.append(jnp.where(lane < part, first, second))
@@ -415,7 +434,7 @@
         in_specs=[whole()] * 4,
         out_specs=[whole(), whole()],
         out_shape=[
-            jax.ShapeDtypeStruct((rows, LANES), f32),
+            jax.ShapeDtypeStruct((slab_count, pencil_count, z_local, LANES), f32),
             jax.ShapeDtypeStruct((8, LANES), f32),
         ],
         scratch_shapes=[
@@ -451,12 +470,16 @@
             scale=grid_mixing / cell_total,
         ),
         in_specs=[scalars()] + [whole()] * 5,
-        out_specs=whole(),
+        out_specs=pl.BlockSpec(memory_space=pltpu.HBM),
         out_shape=jax.ShapeDtypeStruct((slab_count, pencil_count, z_local, LANES), f32),
+        scratch_shapes=[
+            pltpu.VMEM((slab_count, pencil_count, z_local, LANES), f32),
+            pltpu.SemaphoreType.DMA((2 * pencil_count,)),
+        ],
         compiler_params=params(32),
         name="plane",
     )(place, moved, *z_table, *y_table)
-    moved = exchange(packed).reshape(rows, LANES)
+    moved = exchange(packed).reshape(slab_count, pencil_count, z_local, LANES)
     new_density = pl.pallas_call(
         functools.partial(
             x_inverse_kernel, slab_count=slab_count, pencil_count=pencil_count, z_local=z_local

time: 119 us -> 118 us (level)
  no operation moved by 1% of the time
where the time goes in v4:
time: 118 us
  blocking collectives  64.6 us (55%)
  waiting for transfers between devices  25.2 us (21%)
  Pallas kernels  16.7 us (14%)
  starting transfers between devices  6.62 us (6%)
  local copies, waits for them, and re-layouts  2.99 us (3%)
  between operations  1.45 us (1%)
    all_to_all x2, blocking collectives, exchange(): lax.all_to_all(array.reshape(devices, -1, LANES), SLAB_PENCIL, split_axis...  64.6 us
    all_to_all x1, waiting for transfers between devices, exchange(): lax.all_to_all(array.reshape(devices, -1, LANES), SLAB_PENCIL, split_axis...  25.2 us
    all_to_all x1, starting transfers between devices, exchange(): lax.all_to_all(array.reshape(devices, -1, LANES), SLAB_PENCIL, split_axis...  6.62 us
    pallas_call x1, Pallas kernels, body(): pl.pallas_call(functools.partial(plane_kernel, x_length=x_length, y_lengt...  5.17 us
    pallas_call x1, Pallas kernels, body(): pl.pallas_call(functools.partial(gram_kernel, cell_total=cell_total, bloc...  4.63 us
    unnamed x20, local copies, waits for them, and re-layouts  2.99 us
    pallas_call x1, Pallas kernels, body(): pl.pallas_call(mean_kernel, grid=(z_local,), in_specs=[scalars(), scalars...  2.67 us
  transfers between devices with their start and end apart: 1, of which 1 were waited for; matrix products, arithmetic and copies ran while one was open for 0% of the time, Pallas kernels for 2%

profile of v4, /device:TPU:1, one launch (start us, length us, event | category | flops | bytes accessed | tf_op | source)
XLA Modules:
  0.0 117.6 jit_solution(17794359441828135159)
XLA Ops:
  0.6 0.0 copy-start.2
  0.6 0.0 copy-start.3
  1.4 0.1 pad_add_fusion.place_ref
  1.4 0.0 copy-start.4
  1.4 0.0 copy-start.5
  1.4 0.0 copy-start.6
  1.4 0.0 copy-start.7
  1.4 4.6 %gram.1 = (f32[256,128]{1,0:T(8,128)S(1)}, f32[7,8,80,320]{3,2,1,0:T(8,128)S(1)}) custom-call(s32[24]{0:T(128)} %species_ref.1, s32[1]{0:T(128)S(6)} %copy.15.count_ref, f32[7,8,80,320]{3,2,1,0:T(8,128)} %residual_ref.1, f32[7,24,324]{2,1,0:T(8,128)} %block_residual_ref.1), custom_call_target="tpu_custom_call" | custom-call | tf_op jit(solution)/shard_map/gram/pallas_call | solution.py:408
  6.1 28.2 %all_to_all.15 = f32[256,1,128]{2,1,0:T(1,128)S(1)} all-to-all(f32[256,1,128]{2,1,0:T(1,128)S(1)} %bitcast.17), channel_id=1, replica_groups=mesh['slab_0'=8,'slab_1'=4,'slab_2'=2,'pencil'=4] {'slab_0','slab_1','sl..., dimensions={0} | all-to-all | bytes 262144 | tf_op jit(solution)/shard_map/all_to_all | solution.py:427
  34.3 0.0 copy-done.2
  34.3 0.0 copy-done.3
  34.3 0.0 copy-start.1
  34.3 0.0 copy-start.8
  34.3 0.0 copy-start.9
  34.4 1.9 %mix.1 = (f32[64,4,8,128]{3,2,1,0:T(8,128)S(1)}, f32[8,128]{1,0:T(8,128)S(1)}) custom-call(f32[256,128]{1,0:T(8,128)S(1)} %bitcast.16, f32[7,8,80,320]{3,2,1,0:T(8,128)S(1)} %get-tuple-element.13.residual_ref, bf16[320,320]{1,0:T(8,128)(2,1)S(1)} %copy-done.3, bf16[320,320]{1,0:T(8,128)(2,1)S(1)} %copy-done.2), custom_call_target="tpu_custom_call" | custom-call | tf_op jit(solution)/shard_map/mix/pallas_call | solution.py:432
  36.3 36.3 %all_to_all.16 = f32[256,8,128]{2,1,0:T(8,128)S(1)} all-to-all(f32[256,8,128]{2,1,0:T(8,128)S(1)} %bitcast.14), channel_id=1, replica_groups=mesh['slab_0'=8,'slab_1'=4,'slab_2'=2,'pencil'=4] {'slab_0','slab_1','sl..., dimensions={0} | all-to-all | bytes 2097152 | tf_op jit(solution)/shard_map/all_to_all | solution.py:427
  72.6 0.0 copy-done.4
  72.6 0.0 copy-done.5
  72.6 0.0 copy-done.6
  72.7 0.0 copy-done.7
  72.7 5.2 %plane.1 = f32[64,4,8,128]{3,2,1,0:T(8,128)} custom-call(s32[2]{0:T(128)S(1)} %pad_add_fusion.place_ref, f32[64,4,8,128]{3,2,1,0:T(8,128)S(1)} %bitcast.12, bf16[2,256,256]{2,1,0:T(8,128)(2,1)S(1)} %copy-done.7, bf16[2,256,256]{2,1,0:T(8,128)(2,1)S(1)} %copy-done.6, bf16[4,256,320]{2,1,0:T(8,128)(2,1)S(1)} %copy-done.5, bf16[4,256,320]{2,1,0:T(8,128)(2,1)S(1)} %copy-done.4), custom_call_target="tpu_custom_call" | custom-call | tf_op jit(solution)/shard_map/plane/pallas_call | solution.py:464
  77.8 6.6 %all-to-all-start.2 = ((f32[256,8,128]{2,1,0:T(8,128)}), f32[256,8,128]{2,1,0:T(8,128)S(1)}, u32[]{:S(2)}, u32[]{:S(2)}) async-start(f32[256,8,128]{2,1,0:T(8,128)} %bitcast.7), calls=%async_computation.2 | async-start | bytes 2097152 | tf_op jit(solution)/shard_map/all_to_all | solution.py:427
  84.5 0.0 copy-done.1
  84.5 0.0 copy-done.8
  84.5 0.0 copy-done.9
  84.5 0.0 copy-start
  84.5 2.9 %copy-done = f32[7,8,80,320]{3,2,1,0:T(8,128)S(1)} copy-done((f32[7,8,80,320]{3,2,1,0:T(8,128)S(1)}, f32[7,8,80,320]{3,2,1,0:T(8,128)}, u32[]{:S(2)}) %copy-start) | copy-done | bytes 5734424
  87.4 2.7 %mean.1 = (f32[8,80,320]{2,1,0:T(8,128)S(1)}, f32[24,324]{1,0:T(8,128)}) custom-call(s32[24]{0:T(128)S(1)} %copy-done.9, s32[1]{0:T(128)S(6)} %copy.15.count_ref, f32[8,128]{1,0:T(8,128)S(1)} %get-tuple-element.15.weights_ref, f32[7,8,80,320]{3,2,1,0:T(8,128)S(1)} %copy-done, f32[7,24,324]{2,1,0:T(8,128)S(1)} %copy-done.8, f32[7,24,324]{2,1,0:T(8,128)S(1)} %copy-done.1), custom_call_target="tpu_custom_call" | custom-call | tf_op jit(solution)/shard_map/mean/pallas_call | solution.py:449
  90.1 25.2 %all-to-all-done.2 = f32[256,8,128]{2,1,0:T(8,128)S(1)} async-done(((f32[256,8,128]{2,1,0:T(8,128)}), f32[256,8,128]{2,1,0:T(8,128)S(1)}, u32[]{:S(2)}, u32[]{:S(2)}) %all-to-all-start.2) | async-done | bytes 1048608 | tf_op jit(solution)/shard_map/all_to_all | solution.py:427
  115.3 2.3 %x_inverse.1 = f32[640,320]{1,0:T(8,128)} custom-call(f32[64,4,8,128]{3,2,1,0:T(8,128)S(1)} %bitcast.13, f32[640,320]{1,0:T(8,128)S(1)} %bitcast.15, bf16[320,320]{1,0:T(8,128)(2,1)S(1)} %copy-done.3, bf16[320,320]{1,0:T(8,128)(2,1)S(1)} %copy-done.2), custom_call_target="tpu_custom_call" | custom-call | tf_op jit(solution)/shard_map/x_inverse/pallas_call | solution.py:483
Async XLA Ops:
  0.6 33.7 %copy-start.2 = (bf16[320,320]{1,0:T(8,128)(2,1)S(1)}, bf16[320,320]{1,0:T(8,128)(2,1)}, u32[]{:S(2)}) copy-start(bf16[320,320]{1,0:T(8,128)(2,1)} %constant.34.clone.low_ref) | copy-start | bytes 614404
  0.6 33.7 %copy-start.3 = (bf16[320,320]{1,0:T(8,128)(2,1)S(1)}, bf16[320,320]{1,0:T(8,128)(2,1)}, u32[]{:S(2)}) copy-start(bf16[320,320]{1,0:T(8,128)(2,1)} %constant.33.clone.high_ref) | copy-start | bytes 614404
  1.4 71.2 %copy-start.4 = (bf16[4,256,320]{2,1,0:T(8,128)(2,1)S(1)}, bf16[4,256,320]{2,1,0:T(8,128)(2,1)}, u32[]{:S(2)}) copy-start(bf16[4,256,320]{2,1,0:T(8,128)(2,1)} %constant.38.clone.yl_ref) | copy-start | bytes 1966084
  1.4 71.2 %copy-start.5 = (bf16[4,256,320]{2,1,0:T(8,128)(2,1)S(1)}, bf16[4,256,320]{2,1,0:T(8,128)(2,1)}, u32[]{:S(2)}) copy-start(bf16[4,256,320]{2,1,0:T(8,128)(2,1)} %constant.37.clone.yh_ref) | copy-start | bytes 1966084
  1.4 71.2 %copy-start.6 = (bf16[2,256,256]{2,1,0:T(8,128)(2,1)S(1)}, bf16[2,256,256]{2,1,0:T(8,128)(2,1)}, u32[]{:S(2)}) copy-start(bf16[2,256,256]{2,1,0:T(8,128)(2,1)} %constant.36.clone.zl_ref) | copy-start | bytes 786436
  1.4 71.2 %copy-start.7 = (bf16[2,256,256]{2,1,0:T(8,128)(2,1)S(1)}, bf16[2,256,256]{2,1,0:T(8,128)(2,1)}, u32[]{:S(2)}) copy-start(bf16[2,256,256]{2,1,0:T(8,128)(2,1)} %constant.35.clone.zh_ref) | copy-start | bytes 786436
  34.3 50.1 %copy-start.1 = (f32[7,24,324]{2,1,0:T(8,128)S(1)}, f32[7,24,324]{2,1,0:T(8,128)}, u32[]{:S(2)}) copy-start(f32[7,24,324]{2,1,0:T(8,128)} %block_residual_ref.1) | copy-start | bytes 653188
  34.3 50.1 %copy-start.8 = (f32[7,24,324]{2,1,0:T(8,128)S(1)}, f32[7,24,324]{2,1,0:T(8,128)}, u32[]{:S(2)}) copy-start(f32[7,24,324]{2,1,0:T(8,128)} %block_ref.3) | copy-start | bytes 653188
  34.3 50.1 %copy-start.9 = (s32[24]{0:T(128)S(1)}, s32[24]{0:T(128)}, u32[]{:S(2)}) copy-start(s32[24]{0:T(128)} %species_ref.1) | copy-start | bytes 292
  77.8 37.5 %all-to-all-start.2 = ((f32[256,8,128]{2,1,0:T(8,128)}), f32[256,8,128]{2,1,0:T(8,128)S(1)}, u32[]{:S(2)}, u32[]{:S(2)}) async-start(f32[256,8,128]{2,1,0:T(8,128)} %bitcast.7), calls=%async_computation.2 | async-start | bytes 2097152 | tf_op jit(solution)/shard_map/all_to_all | solution.py:427
  84.5 3.0 %copy-start = (f32[7,8,80,320]{3,2,1,0:T(8,128)S(1)}, f32[7,8,80,320]{3,2,1,0:T(8,128)}, u32[]{:S(2)}) copy-start(f32[7,8,80,320]{3,2,1,0:T(8,128)} %density_ref.1) | copy-start | bytes 17203204

commit v5 on v4

--- a/solution.py
+++ b/solution.py
@@ -38,7 +38,10 @@
     dot = functools.partial(
         lax.dot_general, dimension_numbers=(dims, ((), ())), preferred_element_type=f32
     )
-    return dot(left[0], right[0]) + (dot(left[0], right[1]) + dot(left[1], right[0]))
+    axis = 1 - dims[0][0]
+    rows = left[0].shape[axis]
+    both = dot(jnp.concatenate(left, axis=axis), right[0])
+    return both[:rows] + (dot(left[0], right[1]) + both[rows:])
 
 
 def hartley(rows, columns, length):
@@ -250,16 +253,21 @@
         least = jnp.minimum(index, length - index).astype(f32)
         return least * least
 
-    results = []
+    kept = []
     for kind in range(2):
         spectrum = product(split(folded[kind]), y_table(in_half, kind), ((1,), (0,)))
         freq_y = 2 * jnp.where(lane < y_half, lane, lane - y_half) + kind
         square = squared(freq_z, z_length) + (
             squared(freq_y, y_length) + squared(freq_x, x_length)
         )
-        kept = spectrum * (square / (square + kerker_wave * kerker_wave) * scale)
-        results.append(product(split(kept), y_table(out_half, kind), ((1,), (1,))))
-    lines = jnp.concatenate([results[0] + results[1], results[0] - results[1]], axis=1)
+        kept.append(spectrum * (square / (square + kerker_wave * kerker_wave) * scale))
+    parts = []
+    for rows in (slice(0, z_half), slice(z_half, z_length)):
+        results = [
+            product(split(kept[kind][rows]), y_table(out_half, kind), ((1,), (1,)))
+            for kind in range(2)
+        ]
+        parts.append(split(jnp.concatenate([results[0] + results[1], results[0] - results[1]], axis=1)))
     sends = []
     for q in range(pencil_count):
         for first in (0, s_half):
@@ -269,17 +277,15 @@
                     made_ref.at[here, q], out_ref.at[here, q], sent.at[len(sends)]
                 )
             )
-    for start in range(0, pencil_count, 2):
-        columns = slice(start * LANES, (start + 2) * LANES)
-        even = product(z_table(0), split(lines[:z_half, columns]), ((1,), (0,)))
-        odd = product(z_table(1), split(lines[z_half:, columns]), ((0,), (0,)))
-        low, high = even + odd, even - odd
-        for q in (start, start + 1):
-            columns = slice((q - start) * LANES, (q - start + 1) * LANES)
-            made_ref[:s_half, q] = low[:, columns].reshape(s_half, z_local, LANES)
-            sends[2 * q].start()
-            made_ref[s_half:, q] = high[:, columns].reshape(s_half, z_local, LANES)
-            sends[2 * q + 1].start()
+    even = product(z_table(0), parts[0], ((1,), (0,)))
+    odd = product(z_table(1), parts[1], ((0,), (0,)))
+    low, high = even + odd, even - odd
+    for q in range(pencil_count):
+        columns = slice(q * LANES, (q + 1) * LANES)
+        made_ref[:s_half, q] = low[:, columns].reshape(s_half, z_local, LANES)
+        sends[2 * q].start()
+        made_ref[s_half:, q] = high[:, columns].reshape(s_half, z_local, LANES)
+        sends[2 * q + 1].start()
     for send in sends:
         send.wait()
 

time: 118 us -> 117 us (level)
  no operation moved by 1% of the time
where the time goes in v5:
time: 117 us
  blocking collectives  64.6 us (55%)
  waiting for transfers between devices  25.2 us (22%)
  Pallas kernels  15.7 us (13%)
  starting transfers between devices  6.62 us (6%)
  local copies, waits for them, and re-layouts  2.99 us (3%)
  between operations  1.45 us (1%)
    all_to_all x2, blocking collectives, exchange(): lax.all_to_all(array.reshape(devices, -1, LANES), SLAB_PENCIL, split_axis...  64.6 us
    all_to_all x1, waiting for transfers between devices, exchange(): lax.all_to_all(array.reshape(devices, -1, LANES), SLAB_PENCIL, split_axis...  25.2 us
    all_to_all x1, starting transfers between devices, exchange(): lax.all_to_all(array.reshape(devices, -1, LANES), SLAB_PENCIL, split_axis...  6.62 us
    pallas_call x1, Pallas kernels, body(): pl.pallas_call(functools.partial(gram_kernel, cell_total=cell_total, bloc...  4.63 us
    pallas_call x1, Pallas kernels, body(): pl.pallas_call(functools.partial(plane_kernel, x_length=x_length, y_lengt...  4.34 us
    unnamed x20, local copies, waits for them, and re-layouts  2.99 us
    pallas_call x1, Pallas kernels, body(): pl.pallas_call(mean_kernel, grid=(z_local,), in_specs=[scalars(), scalars...  2.67 us
  transfers between devices with their start and end apart: 1, of which 1 were waited for; matrix products, arithmetic and copies ran while one was open for 0% of the time, Pallas kernels for 2%

profile of v5, /device:TPU:1, one launch (start us, length us, event | category | flops | bytes accessed | tf_op | source)
XLA Modules:
  0.0 116.6 jit_solution(8452043509020522527)
XLA Ops:
  0.6 0.0 copy-start.2
  0.6 0.0 copy-start.3
  1.4 0.1 pad_add_fusion.place_ref
  1.4 0.0 copy-start.4
  1.4 0.0 copy-start.5
  1.4 0.0 copy-start.6
  1.4 0.0 copy-start.7
  1.4 4.6 %gram.1 = (f32[256,128]{1,0:T(8,128)S(1)}, f32[7,8,80,320]{3,2,1,0:T(8,128)S(1)}) custom-call(s32[24]{0:T(128)} %species_ref.1, s32[1]{0:T(128)S(6)} %copy.15.count_ref, f32[7,8,80,320]{3,2,1,0:T(8,128)} %residual_ref.1, f32[7,24,324]{2,1,0:T(8,128)} %block_residual_ref.1), custom_call_target="tpu_custom_call" | custom-call | tf_op jit(solution)/shard_map/gram/pallas_call | solution.py:414
  6.1 28.2 %all_to_all.15 = f32[256,1,128]{2,1,0:T(1,128)S(1)} all-to-all(f32[256,1,128]{2,1,0:T(1,128)S(1)} %bitcast.17), channel_id=1, replica_groups=mesh['slab_0'=8,'slab_1'=4,'slab_2'=2,'pencil'=4] {'slab_0','slab_1','sl..., dimensions={0} | all-to-all | bytes 262144 | tf_op jit(solution)/shard_map/all_to_all | solution.py:433
  34.3 0.0 copy-done.2
  34.3 0.0 copy-done.3
  34.3 0.0 copy-start.1
  34.3 0.0 copy-start.8
  34.3 0.0 copy-start.9
  34.4 1.8 %mix.1 = (f32[64,4,8,128]{3,2,1,0:T(8,128)S(1)}, f32[8,128]{1,0:T(8,128)S(1)}) custom-call(f32[256,128]{1,0:T(8,128)S(1)} %bitcast.16, f32[7,8,80,320]{3,2,1,0:T(8,128)S(1)} %get-tuple-element.13.residual_ref, bf16[320,320]{1,0:T(8,128)(2,1)S(1)} %copy-done.3, bf16[320,320]{1,0:T(8,128)(2,1)S(1)} %copy-done.2), custom_call_target="tpu_custom_call" | custom-call | tf_op jit(solution)/shard_map/mix/pallas_call | solution.py:438
  36.2 36.3 %all_to_all.16 = f32[256,8,128]{2,1,0:T(8,128)S(1)} all-to-all(f32[256,8,128]{2,1,0:T(8,128)S(1)} %bitcast.14), channel_id=1, replica_groups=mesh['slab_0'=8,'slab_1'=4,'slab_2'=2,'pencil'=4] {'slab_0','slab_1','sl..., dimensions={0} | all-to-all | bytes 2097152 | tf_op jit(solution)/shard_map/all_to_all | solution.py:433
  72.5 0.0 copy-done.4
  72.6 0.0 copy-done.5
  72.6 0.0 copy-done.6
  72.6 0.0 copy-done.7
  72.6 4.3 %plane.1 = f32[64,4,8,128]{3,2,1,0:T(8,128)} custom-call(s32[2]{0:T(128)S(1)} %pad_add_fusion.place_ref, f32[64,4,8,128]{3,2,1,0:T(8,128)S(1)} %bitcast.12, bf16[2,256,256]{2,1,0:T(8,128)(2,1)S(1)} %copy-done.7, bf16[2,256,256]{2,1,0:T(8,128)(2,1)S(1)} %copy-done.6, bf16[4,256,320]{2,1,0:T(8,128)(2,1)S(1)} %copy-done.5, bf16[4,256,320]{2,1,0:T(8,128)(2,1)S(1)} %copy-done.4), custom_call_target="tpu_custom_call" | custom-call | tf_op jit(solution)/shard_map/plane/pallas_call | solution.py:470
  76.9 6.6 %all-to-all-start.2 = ((f32[256,8,128]{2,1,0:T(8,128)}), f32[256,8,128]{2,1,0:T(8,128)S(1)}, u32[]{:S(2)}, u32[]{:S(2)}) async-start(f32[256,8,128]{2,1,0:T(8,128)} %bitcast.7), calls=%async_computation.2 | async-start | bytes 2097152 | tf_op jit(solution)/shard_map/all_to_all | solution.py:433
  83.5 0.0 copy-done.1
  83.6 0.0 copy-done.8
  83.6 0.0 copy-done.9
  83.6 0.0 copy-start
  83.6 2.9 %copy-done = f32[7,8,80,320]{3,2,1,0:T(8,128)S(1)} copy-done((f32[7,8,80,320]{3,2,1,0:T(8,128)S(1)}, f32[7,8,80,320]{3,2,1,0:T(8,128)}, u32[]{:S(2)}) %copy-start) | copy-done | bytes 5734424
  86.5 2.7 %mean.1 = (f32[8,80,320]{2,1,0:T(8,128)S(1)}, f32[24,324]{1,0:T(8,128)}) custom-call(s32[24]{0:T(128)S(1)} %copy-done.9, s32[1]{0:T(128)S(6)} %copy.15.count_ref, f32[8,128]{1,0:T(8,128)S(1)} %get-tuple-element.15.weights_ref, f32[7,8,80,320]{3,2,1,0:T(8,128)S(1)} %copy-done, f32[7,24,324]{2,1,0:T(8,128)S(1)} %copy-done.8, f32[7,24,324]{2,1,0:T(8,128)S(1)} %copy-done.1), custom_call_target="tpu_custom_call" | custom-call | tf_op jit(solution)/shard_map/mean/pallas_call | solution.py:455
  89.2 25.2 %all-to-all-done.2 = f32[256,8,128]{2,1,0:T(8,128)S(1)} async-done(((f32[256,8,128]{2,1,0:T(8,128)}), f32[256,8,128]{2,1,0:T(8,128)S(1)}, u32[]{:S(2)}, u32[]{:S(2)}) %all-to-all-start.2) | async-done | bytes 1048608 | tf_op jit(solution)/shard_map/all_to_all | solution.py:433
  114.4 2.2 %x_inverse.1 = f32[640,320]{1,0:T(8,128)} custom-call(f32[64,4,8,128]{3,2,1,0:T(8,128)S(1)} %bitcast.13, f32[640,320]{1,0:T(8,128)S(1)} %bitcast.15, bf16[320,320]{1,0:T(8,128)(2,1)S(1)} %copy-done.3, bf16[320,320]{1,0:T(8,128)(2,1)S(1)} %copy-done.2), custom_call_target="tpu_custom_call" | custom-call | tf_op jit(solution)/shard_map/x_inverse/pallas_call | solution.py:489
Async XLA Ops:
  0.6 33.7 %copy-start.2 = (bf16[320,320]{1,0:T(8,128)(2,1)S(1)}, bf16[320,320]{1,0:T(8,128)(2,1)}, u32[]{:S(2)}) copy-start(bf16[320,320]{1,0:T(8,128)(2,1)} %constant.34.clone.low_ref) | copy-start | bytes 614404
  0.6 33.7 %copy-start.3 = (bf16[320,320]{1,0:T(8,128)(2,1)S(1)}, bf16[320,320]{1,0:T(8,128)(2,1)}, u32[]{:S(2)}) copy-start(bf16[320,320]{1,0:T(8,128)(2,1)} %constant.33.clone.high_ref) | copy-start | bytes 614404
  1.4 71.1 %copy-start.4 = (bf16[4,256,320]{2,1,0:T(8,128)(2,1)S(1)}, bf16[4,256,320]{2,1,0:T(8,128)(2,1)}, u32[]{:S(2)}) copy-start(bf16[4,256,320]{2,1,0:T(8,128)(2,1)} %constant.38.clone.yl_ref) | copy-start | bytes 1966084
  1.4 71.1 %copy-start.5 = (bf16[4,256,320]{2,1,0:T(8,128)(2,1)S(1)}, bf16[4,256,320]{2,1,0:T(8,128)(2,1)}, u32[]{:S(2)}) copy-start(bf16[4,256,320]{2,1,0:T(8,128)(2,1)} %constant.37.clone.yh_ref) | copy-start | bytes 1966084
  1.4 71.1 %copy-start.6 = (bf16[2,256,256]{2,1,0:T(8,128)(2,1)S(1)}, bf16[2,256,256]{2,1,0:T(8,128)(2,1)}, u32[]{:S(2)}) copy-start(bf16[2,256,256]{2,1,0:T(8,128)(2,1)} %constant.36.clone.zl_ref) | copy-start | bytes 786436
  1.4 71.1 %copy-start.7 = (bf16[2,256,256]{2,1,0:T(8,128)(2,1)S(1)}, bf16[2,256,256]{2,1,0:T(8,128)(2,1)}, u32[]{:S(2)}) copy-start(bf16[2,256,256]{2,1,0:T(8,128)(2,1)} %constant.35.clone.zh_ref) | copy-start | bytes 786436
  34.3 49.2 %copy-start.1 = (f32[7,24,324]{2,1,0:T(8,128)S(1)}, f32[7,24,324]{2,1,0:T(8,128)}, u32[]{:S(2)}) copy-start(f32[7,24,324]{2,1,0:T(8,128)} %block_residual_ref.1) | copy-start | bytes 653188
  34.3 49.2 %copy-start.8 = (f32[7,24,324]{2,1,0:T(8,128)S(1)}, f32[7,24,324]{2,1,0:T(8,128)}, u32[]{:S(2)}) copy-start(f32[7,24,324]{2,1,0:T(8,128)} %block_ref.3) | copy-start | bytes 653188
  34.3 49.2 %copy-start.9 = (s32[24]{0:T(128)S(1)}, s32[24]{0:T(128)}, u32[]{:S(2)}) copy-start(s32[24]{0:T(128)} %species_ref.1) | copy-start | bytes 292
  76.9 37.5 %all-to-all-start.2 = ((f32[256,8,128]{2,1,0:T(8,128)}), f32[256,8,128]{2,1,0:T(8,128)S(1)}, u32[]{:S(2)}, u32[]{:S(2)}) async-start(f32[256,8,128]{2,1,0:T(8,128)} %bitcast.7), calls=%async_computation.2 | async-start | bytes 2097152 | tf_op jit(solution)/shard_map/all_to_all | solution.py:433
  83.6 3.0 %copy-start = (f32[7,8,80,320]{3,2,1,0:T(8,128)S(1)}, f32[7,8,80,320]{3,2,1,0:T(8,128)}, u32[]{:S(2)}) copy-start(f32[7,8,80,320]{3,2,1,0:T(8,128)} %density_ref.1) | copy-start | bytes 17203204

commit v6 on v5

--- a/solution.py
+++ b/solution.py
@@ -69,14 +69,17 @@
 
 
 def gram_kernel(
-    species_ref,
+    species_source,
     count_ref,
     residual_ref,
-    block_ref,
+    block_source,
     out_ref,
     held_ref,
     acc_ref,
+    species_ref,
+    block_ref,
     arrived,
+    small_arrived,
     *,
     cell_total,
     block_total,
@@ -87,9 +90,22 @@
     def fetch(z):
         return pltpu.make_async_copy(residual_ref.at[:, z], held_ref.at[:, z], arrived.at[z])
 
+    small = [
+        pltpu.make_async_copy(source, target, small_arrived.at[index])
+        for index, (source, target) in enumerate(
+            (
+                (species_source, species_ref),
+                (block_source, block_ref),
+            )
+        )
+    ]
+    for copy in small:
+        copy.start()
     for z in range(planes):
         fetch(z).start()
     acc_ref[...] = jnp.zeros_like(acc_ref)
+    for copy in small:
+        copy.wait()
     _, slots, entries = block_ref.shape
     mask = block_mask(species_ref, count_ref, slots, entries)
     blocks = [jnp.where(mask, block_ref[i], 0.0) for i in range(histories)]
@@ -101,14 +117,28 @@
 
     def plane(z, carry):
         fetch(z).wait()
-        for start in range(0, width, LANES):
-            lanes = slice(start, min(start + LANES, width))
+        body_width = width // LANES * LANES
+        for start in range(0, body_width, LANES):
+            lanes = slice(start, start + LANES)
             accs = [acc_ref[k, :, lanes] for k in range(len(pairs))]
             for top in range(0, rows, 8):
                 values = [held_ref[i, z, top : top + 8, lanes] for i in range(histories)]
                 accs = [acc + values[i] * values[j] for acc, (i, j) in zip(accs, pairs)]
             for k, acc in enumerate(accs):
                 acc_ref[k, :, lanes] = acc
+        lanes = slice(body_width, width)
+        accs = [acc_ref[k, :, body_width:] for k in range(len(pairs))]
+        for top in range(0, rows, 16):
+            values = [
+                jnp.concatenate(
+                    [held_ref[i, z, top : top + 8, lanes], held_ref[i, z, top + 8 : top + 16, lanes]],
+                    axis=1,
+                )
+                for i in range(histories)
+            ]
+            accs = [acc + values[i] * values[j] for acc, (i, j) in zip(accs, pairs)]
+        for k, acc in enumerate(accs):
+            acc_ref[k, :, body_width:] = acc
         return carry
 
     lax.fori_loop(0, planes, plane, 0)
@@ -411,19 +441,23 @@
     place = jnp.stack([lax.axis_index(SLAB), lax.axis_index("pencil")]).astype(jnp.int32)
     place, species = lax.optimization_barrier((place, species))
 
+    in_place = pl.BlockSpec(memory_space=pltpu.HBM)
     sums, held = pl.pallas_call(
         functools.partial(
             gram_kernel, cell_total=cell_total, block_total=100.0 * slots * devices
         ),
-        in_specs=[scalars(), scalars(), pl.BlockSpec(memory_space=pltpu.HBM), whole()],
+        in_specs=[in_place, scalars(), in_place, in_place],
         out_specs=[whole(), whole()],
         out_shape=[
             jax.ShapeDtypeStruct((devices, LANES), f32),
             jax.ShapeDtypeStruct(residual_history.shape, f32),
         ],
         scratch_shapes=[
-            pltpu.VMEM((len(pair_list(histories)), 8, x_length), f32),
+            pltpu.VMEM((len(pair_list(histories)), 8, -(-x_length // LANES) * LANES), f32),
+            pltpu.SMEM(species.shape, jnp.int32),
+            pltpu.VMEM(occupancy_residual.shape, f32),
             pltpu.SemaphoreType.DMA((z_local,)),
+            pltpu.SemaphoreType.DMA((2,)),
         ],
         compiler_params=params(16),
         name="gram",

time: 117 us -> 117 us (level)
  no operation moved by 1% of the time
where the time goes in v6:
time: 117 us
  blocking collectives  64.6 us (55%)
  waiting for transfers between devices  25.2 us (22%)
  Pallas kernels  16.1 us (14%)
  starting transfers between devices  6.62 us (6%)
  local copies, waits for them, and re-layouts  2.99 us (3%)
  between operations  1.45 us (1%)
    all_to_all x2, blocking collectives, exchange(): lax.all_to_all(array.reshape(devices, -1, LANES), SLAB_PENCIL, split_axis...  64.6 us
    all_to_all x1, waiting for transfers between devices, exchange(): lax.all_to_all(array.reshape(devices, -1, LANES), SLAB_PENCIL, split_axis...  25.2 us
    all_to_all x1, starting transfers between devices, exchange(): lax.all_to_all(array.reshape(devices, -1, LANES), SLAB_PENCIL, split_axis...  6.62 us
    pallas_call x1, Pallas kernels, body(): pl.pallas_call(functools.partial(gram_kernel, cell_total=cell_total, bloc...  5.01 us
    pallas_call x1, Pallas kernels, body(): pl.pallas_call(functools.partial(plane_kernel, x_length=x_length, y_lengt...  4.34 us
    unnamed x20, local copies, waits for them, and re-layouts  2.99 us
    pallas_call x1, Pallas kernels, body(): pl.pallas_call(mean_kernel, grid=(z_local,), in_specs=[scalars(), scalars...  2.67 us
  transfers between devices with their start and end apart: 1, of which 1 were waited for; matrix products, arithmetic and copies ran while one was open for 0% of the time, Pallas kernels for 2%

profile of v6, /device:TPU:1, one launch (start us, length us, event | category | flops | bytes accessed | tf_op | source)
XLA Modules:
  0.0 117.0 jit_solution(4347192759369131249)
XLA Ops:
  0.6 0.0 copy-start.2
  0.6 0.0 copy-start.3
  1.4 0.1 pad_add_fusion.place_ref
  1.4 0.0 copy-start.4
  1.4 0.0 copy-start.5
  1.4 0.0 copy-start.6
  1.4 0.0 copy-start.7
  1.4 5.0 %gram.1 = (f32[256,128]{1,0:T(8,128)S(1)}, f32[7,8,80,320]{3,2,1,0:T(8,128)S(1)}) custom-call(s32[24]{0:T(128)} %species_ref, s32[1]{0:T(128)S(6)} %copy.15.count_ref, f32[7,8,80,320]{3,2,1,0:T(8,128)} %residual_ref.1, f32[7,24,324]{2,1,0:T(8,128)} %block_residual_ref.1), custom_call_target="tpu_custom_call" | custom-call | tf_op jit(solution)/shard_map/gram/pallas_call | solution.py:445
  6.5 28.2 %all_to_all.15 = f32[256,1,128]{2,1,0:T(1,128)S(1)} all-to-all(f32[256,1,128]{2,1,0:T(1,128)S(1)} %bitcast.17), channel_id=1, replica_groups=mesh['slab_0'=8,'slab_1'=4,'slab_2'=2,'pencil'=4] {'slab_0','slab_1','sl..., dimensions={0} | all-to-all | bytes 262144 | tf_op jit(solution)/shard_map/all_to_all | solution.py:467
  34.7 0.0 copy-done.2
  34.7 0.0 copy-done.3
  34.7 0.0 copy-start.1
  34.7 0.0 copy-start.8
  34.7 0.0 copy-start.9
  34.7 1.8 %mix.1 = (f32[64,4,8,128]{3,2,1,0:T(8,128)S(1)}, f32[8,128]{1,0:T(8,128)S(1)}) custom-call(f32[256,128]{1,0:T(8,128)S(1)} %bitcast.16, f32[7,8,80,320]{3,2,1,0:T(8,128)S(1)} %get-tuple-element.13.residual_ref, bf16[320,320]{1,0:T(8,128)(2,1)S(1)} %copy-done.3, bf16[320,320]{1,0:T(8,128)(2,1)S(1)} %copy-done.2), custom_call_target="tpu_custom_call" | custom-call | tf_op jit(solution)/shard_map/mix/pallas_call | solution.py:472
  36.6 36.3 %all_to_all.16 = f32[256,8,128]{2,1,0:T(8,128)S(1)} all-to-all(f32[256,8,128]{2,1,0:T(8,128)S(1)} %bitcast.14), channel_id=1, replica_groups=mesh['slab_0'=8,'slab_1'=4,'slab_2'=2,'pencil'=4] {'slab_0','slab_1','sl..., dimensions={0} | all-to-all | bytes 2097152 | tf_op jit(solution)/shard_map/all_to_all | solution.py:467
  72.9 0.0 copy-done.4
  72.9 0.0 copy-done.5
  72.9 0.0 copy-done.6
  72.9 0.0 copy-done.7
  73.0 4.3 %plane.1 = f32[64,4,8,128]{3,2,1,0:T(8,128)} custom-call(s32[2]{0:T(128)S(1)} %pad_add_fusion.place_ref, f32[64,4,8,128]{3,2,1,0:T(8,128)S(1)} %bitcast.12, bf16[2,256,256]{2,1,0:T(8,128)(2,1)S(1)} %copy-done.7, bf16[2,256,256]{2,1,0:T(8,128)(2,1)S(1)} %copy-done.6, bf16[4,256,320]{2,1,0:T(8,128)(2,1)S(1)} %copy-done.5, bf16[4,256,320]{2,1,0:T(8,128)(2,1)S(1)} %copy-done.4), custom_call_target="tpu_custom_call" | custom-call | tf_op jit(solution)/shard_map/plane/pallas_call | solution.py:504
  77.3 6.6 %all-to-all-start.2 = ((f32[256,8,128]{2,1,0:T(8,128)}), f32[256,8,128]{2,1,0:T(8,128)S(1)}, u32[]{:S(2)}, u32[]{:S(2)}) async-start(f32[256,8,128]{2,1,0:T(8,128)} %bitcast.7), calls=%async_computation.2 | async-start | bytes 2097152 | tf_op jit(solution)/shard_map/all_to_all | solution.py:467
  83.9 0.0 copy-done.1
  83.9 0.0 copy-done.8
  84.0 0.0 copy-done.9
  84.0 0.0 copy-start
  84.0 2.9 %copy-done = f32[7,8,80,320]{3,2,1,0:T(8,128)S(1)} copy-done((f32[7,8,80,320]{3,2,1,0:T(8,128)S(1)}, f32[7,8,80,320]{3,2,1,0:T(8,128)}, u32[]{:S(2)}) %copy-start) | copy-done | bytes 5734424
  86.9 2.7 %mean.1 = (f32[8,80,320]{2,1,0:T(8,128)S(1)}, f32[24,324]{1,0:T(8,128)}) custom-call(s32[24]{0:T(128)S(1)} %copy-done.9, s32[1]{0:T(128)S(6)} %copy.15.count_ref, f32[8,128]{1,0:T(8,128)S(1)} %get-tuple-element.15.weights_ref, f32[7,8,80,320]{3,2,1,0:T(8,128)S(1)} %copy-done, f32[7,24,324]{2,1,0:T(8,128)S(1)} %copy-done.8, f32[7,24,324]{2,1,0:T(8,128)S(1)} %copy-done.1), custom_call_target="tpu_custom_call" | custom-call | tf_op jit(solution)/shard_map/mean/pallas_call | solution.py:489
  89.6 25.2 %all-to-all-done.2 = f32[256,8,128]{2,1,0:T(8,128)S(1)} async-done(((f32[256,8,128]{2,1,0:T(8,128)}), f32[256,8,128]{2,1,0:T(8,128)S(1)}, u32[]{:S(2)}, u32[]{:S(2)}) %all-to-all-start.2) | async-done | bytes 1048608 | tf_op jit(solution)/shard_map/all_to_all | solution.py:467
  114.8 2.2 %x_inverse.1 = f32[640,320]{1,0:T(8,128)} custom-call(f32[64,4,8,128]{3,2,1,0:T(8,128)S(1)} %bitcast.13, f32[640,320]{1,0:T(8,128)S(1)} %bitcast.15, bf16[320,320]{1,0:T(8,128)(2,1)S(1)} %copy-done.3, bf16[320,320]{1,0:T(8,128)(2,1)S(1)} %copy-done.2), custom_call_target="tpu_custom_call" | custom-call | tf_op jit(solution)/shard_map/x_inverse/pallas_call | solution.py:523
Async XLA Ops:
  0.6 34.1 %copy-start.2 = (bf16[320,320]{1,0:T(8,128)(2,1)S(1)}, bf16[320,320]{1,0:T(8,128)(2,1)}, u32[]{:S(2)}) copy-start(bf16[320,320]{1,0:T(8,128)(2,1)} %constant.34.clone.low_ref) | copy-start | bytes 614404
  0.6 34.1 %copy-start.3 = (bf16[320,320]{1,0:T(8,128)(2,1)S(1)}, bf16[320,320]{1,0:T(8,128)(2,1)}, u32[]{:S(2)}) copy-start(bf16[320,320]{1,0:T(8,128)(2,1)} %constant.33.clone.high_ref) | copy-start | bytes 614404
  1.4 71.5 %copy-start.4 = (bf16[4,256,320]{2,1,0:T(8,128)(2,1)S(1)}, bf16[4,256,320]{2,1,0:T(8,128)(2,1)}, u32[]{:S(2)}) copy-start(bf16[4,256,320]{2,1,0:T(8,128)(2,1)} %constant.38.clone.yl_ref) | copy-start | bytes 1966084
  1.4 71.5 %copy-start.5 = (bf16[4,256,320]{2,1,0:T(8,128)(2,1)S(1)}, bf16[4,256,320]{2,1,0:T(8,128)(2,1)}, u32[]{:S(2)}) copy-start(bf16[4,256,320]{2,1,0:T(8,128)(2,1)} %constant.37.clone.yh_ref) | copy-start | bytes 1966084
  1.4 71.5 %copy-start.6 = (bf16[2,256,256]{2,1,0:T(8,128)(2,1)S(1)}, bf16[2,256,256]{2,1,0:T(8,128)(2,1)}, u32[]{:S(2)}) copy-start(bf16[2,256,256]{2,1,0:T(8,128)(2,1)} %constant.36.clone.zl_ref) | copy-start | bytes 786436
  1.4 71.5 %copy-start.7 = (bf16[2,256,256]{2,1,0:T(8,128)(2,1)S(1)}, bf16[2,256,256]{2,1,0:T(8,128)(2,1)}, u32[]{:S(2)}) copy-start(bf16[2,256,256]{2,1,0:T(8,128)(2,1)} %constant.35.clone.zh_ref) | copy-start | bytes 786436
  34.7 49.2 %copy-start.1 = (f32[7,24,324]{2,1,0:T(8,128)S(1)}, f32[7,24,324]{2,1,0:T(8,128)}, u32[]{:S(2)}) copy-start(f32[7,24,324]{2,1,0:T(8,128)} %block_residual_ref.1) | copy-start | bytes 653188
  34.7 49.2 %copy-start.8 = (f32[7,24,324]{2,1,0:T(8,128)S(1)}, f32[7,24,324]{2,1,0:T(8,128)}, u32[]{:S(2)}) copy-start(f32[7,24,324]{2,1,0:T(8,128)} %block_ref.1) | copy-start | bytes 653188
  34.7 49.2 %copy-start.9 = (s32[24]{0:T(128)S(1)}, s32[24]{0:T(128)}, u32[]{:S(2)}) copy-start(s32[24]{0:T(128)} %species_ref) | copy-start | bytes 292
  77.3 37.5 %all-to-all-start.2 = ((f32[256,8,128]{2,1,0:T(8,128)}), f32[256,8,128]{2,1,0:T(8,128)S(1)}, u32[]{:S(2)}, u32[]{:S(2)}) async-start(f32[256,8,128]{2,1,0:T(8,128)} %bitcast.7), calls=%async_computation.2 | async-start | bytes 2097152 | tf_op jit(solution)/shard_map/all_to_all | solution.py:467
  84.0 3.0 %copy-start = (f32[7,8,80,320]{3,2,1,0:T(8,128)S(1)}, f32[7,8,80,320]{3,2,1,0:T(8,128)}, u32[]{:S(2)}) copy-start(f32[7,8,80,320]{3,2,1,0:T(8,128)} %density_ref.1) | copy-start | bytes 17203204

commit v7 on v5

--- a/solution.py
+++ b/solution.py
@@ -101,14 +101,28 @@
 
     def plane(z, carry):
         fetch(z).wait()
-        for start in range(0, width, LANES):
-            lanes = slice(start, min(start + LANES, width))
+        body_width = width // LANES * LANES
+        for start in range(0, body_width, LANES):
+            lanes = slice(start, start + LANES)
             accs = [acc_ref[k, :, lanes] for k in range(len(pairs))]
             for top in range(0, rows, 8):
                 values = [held_ref[i, z, top : top + 8, lanes] for i in range(histories)]
                 accs = [acc + values[i] * values[j] for acc, (i, j) in zip(accs, pairs)]
             for k, acc in enumerate(accs):
                 acc_ref[k, :, lanes] = acc
+        lanes = slice(body_width, width)
+        accs = [acc_ref[k, :, body_width:] for k in range(len(pairs))]
+        for top in range(0, rows, 16):
+            values = [
+                jnp.concatenate(
+                    [held_ref[i, z, top : top + 8, lanes], held_ref[i, z, top + 8 : top + 16, lanes]],
+                    axis=1,
+                )
+                for i in range(histories)
+            ]
+            accs = [acc + values[i] * values[j] for acc, (i, j) in zip(accs, pairs)]
+        for k, acc in enumerate(accs):
+            acc_ref[k, :, body_width:] = acc
         return carry
 
     lax.fori_loop(0, planes, plane, 0)
@@ -422,7 +436,7 @@
             jax.ShapeDtypeStruct(residual_history.shape, f32),
         ],
         scratch_shapes=[
-            pltpu.VMEM((len(pair_list(histories)), 8, x_length), f32),
+            pltpu.VMEM((len(pair_list(histories)), 8, -(-x_length // LANES) * LANES), f32),
             pltpu.SemaphoreType.DMA((z_local,)),
         ],
         compiler_params=params(16),

time: 117 us -> 117 us (level)
  no operation moved by 1% of the time
where the time goes in v7:
time: 117 us
  blocking collectives  64.6 us (55%)
  waiting for transfers between devices  25.2 us (22%)
  Pallas kernels  15.7 us (13%)
  starting transfers between devices  6.62 us (6%)
  local copies, waits for them, and re-layouts  2.99 us (3%)
  between operations  1.45 us (1%)
    all_to_all x2, blocking collectives, exchange(): lax.all_to_all(array.reshape(devices, -1, LANES), SLAB_PENCIL, split_axis...  64.6 us
    all_to_all x1, waiting for transfers between devices, exchange(): lax.all_to_all(array.reshape(devices, -1, LANES), SLAB_PENCIL, split_axis...  25.2 us
    all_to_all x1, starting transfers between devices, exchange(): lax.all_to_all(array.reshape(devices, -1, LANES), SLAB_PENCIL, split_axis...  6.62 us
    pallas_call x1, Pallas kernels, body(): pl.pallas_call(functools.partial(gram_kernel, cell_total=cell_total, bloc...  4.6 us
    pallas_call x1, Pallas kernels, body(): pl.pallas_call(functools.partial(plane_kernel, x_length=x_length, y_lengt...  4.34 us
    unnamed x20, local copies, waits for them, and re-layouts  2.99 us
    pallas_call x1, Pallas kernels, body(): pl.pallas_call(mean_kernel, grid=(z_local,), in_specs=[scalars(), scalars...  2.67 us
  transfers between devices with their start and end apart: 1, of which 1 were waited for; matrix products, arithmetic and copies ran while one was open for 0% of the time, Pallas kernels for 2%

profile of v7, /device:TPU:1, one launch (start us, length us, event | category | flops | bytes accessed | tf_op | source)
XLA Modules:
  0.0 116.6 jit_solution(8458560968880184369)
XLA Ops:
  0.6 0.0 copy-start.2
  0.6 0.0 copy-start.3
  1.4 0.1 pad_add_fusion.place_ref
  1.4 0.0 copy-start.4
  1.4 0.0 copy-start.5
  1.4 0.0 copy-start.6
  1.4 0.0 copy-start.7
  1.4 4.6 %gram.1 = (f32[256,128]{1,0:T(8,128)S(1)}, f32[7,8,80,320]{3,2,1,0:T(8,128)S(1)}) custom-call(s32[24]{0:T(128)} %species_ref.1, s32[1]{0:T(128)S(6)} %copy.15.count_ref, f32[7,8,80,320]{3,2,1,0:T(8,128)} %residual_ref.1, f32[7,24,324]{2,1,0:T(8,128)} %block_residual_ref.1), custom_call_target="tpu_custom_call" | custom-call | tf_op jit(solution)/shard_map/gram/pallas_call | solution.py:428
  6.1 28.2 %all_to_all.15 = f32[256,1,128]{2,1,0:T(1,128)S(1)} all-to-all(f32[256,1,128]{2,1,0:T(1,128)S(1)} %bitcast.17), channel_id=1, replica_groups=mesh['slab_0'=8,'slab_1'=4,'slab_2'=2,'pencil'=4] {'slab_0','slab_1','sl..., dimensions={0} | all-to-all | bytes 262144 | tf_op jit(solution)/shard_map/all_to_all | solution.py:447
  34.3 0.0 copy-done.2
  34.3 0.0 copy-done.3
  34.3 0.0 copy-start.1
  34.3 0.0 copy-start.8
  34.3 0.0 copy-start.9
  34.3 1.8 %mix.1 = (f32[64,4,8,128]{3,2,1,0:T(8,128)S(1)}, f32[8,128]{1,0:T(8,128)S(1)}) custom-call(f32[256,128]{1,0:T(8,128)S(1)} %bitcast.16, f32[7,8,80,320]{3,2,1,0:T(8,128)S(1)} %get-tuple-element.13.residual_ref, bf16[320,320]{1,0:T(8,128)(2,1)S(1)} %copy-done.3, bf16[320,320]{1,0:T(8,128)(2,1)S(1)} %copy-done.2), custom_call_target="tpu_custom_call" | custom-call | tf_op jit(solution)/shard_map/mix/pallas_call | solution.py:452
  36.2 36.3 %all_to_all.16 = f32[256,8,128]{2,1,0:T(8,128)S(1)} all-to-all(f32[256,8,128]{2,1,0:T(8,128)S(1)} %bitcast.14), channel_id=1, replica_groups=mesh['slab_0'=8,'slab_1'=4,'slab_2'=2,'pencil'=4] {'slab_0','slab_1','sl..., dimensions={0} | all-to-all | bytes 2097152 | tf_op jit(solution)/shard_map/all_to_all | solution.py:447
  72.5 0.0 copy-done.4
  72.5 0.0 copy-done.5
  72.5 0.0 copy-done.6
  72.5 0.0 copy-done.7
  72.5 4.3 %plane.1 = f32[64,4,8,128]{3,2,1,0:T(8,128)} custom-call(s32[2]{0:T(128)S(1)} %pad_add_fusion.place_ref, f32[64,4,8,128]{3,2,1,0:T(8,128)S(1)} %bitcast.12, bf16[2,256,256]{2,1,0:T(8,128)(2,1)S(1)} %copy-done.7, bf16[2,256,256]{2,1,0:T(8,128)(2,1)S(1)} %copy-done.6, bf16[4,256,320]{2,1,0:T(8,128)(2,1)S(1)} %copy-done.5, bf16[4,256,320]{2,1,0:T(8,128)(2,1)S(1)} %copy-done.4), custom_call_target="tpu_custom_call" | custom-call | tf_op jit(solution)/shard_map/plane/pallas_call | solution.py:484
  76.9 6.6 %all-to-all-start.2 = ((f32[256,8,128]{2,1,0:T(8,128)}), f32[256,8,128]{2,1,0:T(8,128)S(1)}, u32[]{:S(2)}, u32[]{:S(2)}) async-start(f32[256,8,128]{2,1,0:T(8,128)} %bitcast.7), calls=%async_computation.2 | async-start | bytes 2097152 | tf_op jit(solution)/shard_map/all_to_all | solution.py:447
  83.5 0.0 copy-done.1
  83.5 0.0 copy-done.8
  83.5 0.0 copy-done.9
  83.6 0.0 copy-start
  83.6 2.9 %copy-done = f32[7,8,80,320]{3,2,1,0:T(8,128)S(1)} copy-done((f32[7,8,80,320]{3,2,1,0:T(8,128)S(1)}, f32[7,8,80,320]{3,2,1,0:T(8,128)}, u32[]{:S(2)}) %copy-start) | copy-done | bytes 5734424
  86.5 2.7 %mean.1 = (f32[8,80,320]{2,1,0:T(8,128)S(1)}, f32[24,324]{1,0:T(8,128)}) custom-call(s32[24]{0:T(128)S(1)} %copy-done.9, s32[1]{0:T(128)S(6)} %copy.15.count_ref, f32[8,128]{1,0:T(8,128)S(1)} %get-tuple-element.15.weights_ref, f32[7,8,80,320]{3,2,1,0:T(8,128)S(1)} %copy-done, f32[7,24,324]{2,1,0:T(8,128)S(1)} %copy-done.8, f32[7,24,324]{2,1,0:T(8,128)S(1)} %copy-done.1), custom_call_target="tpu_custom_call" | custom-call | tf_op jit(solution)/shard_map/mean/pallas_call | solution.py:469
  89.2 25.2 %all-to-all-done.2 = f32[256,8,128]{2,1,0:T(8,128)S(1)} async-done(((f32[256,8,128]{2,1,0:T(8,128)}), f32[256,8,128]{2,1,0:T(8,128)S(1)}, u32[]{:S(2)}, u32[]{:S(2)}) %all-to-all-start.2) | async-done | bytes 1048608 | tf_op jit(solution)/shard_map/all_to_all | solution.py:447
  114.4 2.2 %x_inverse.1 = f32[640,320]{1,0:T(8,128)} custom-call(f32[64,4,8,128]{3,2,1,0:T(8,128)S(1)} %bitcast.13, f32[640,320]{1,0:T(8,128)S(1)} %bitcast.15, bf16[320,320]{1,0:T(8,128)(2,1)S(1)} %copy-done.3, bf16[320,320]{1,0:T(8,128)(2,1)S(1)} %copy-done.2), custom_call_target="tpu_custom_call" | custom-call | tf_op jit(solution)/shard_map/x_inverse/pallas_call | solution.py:503
Async XLA Ops:
  0.6 33.7 %copy-start.2 = (bf16[320,320]{1,0:T(8,128)(2,1)S(1)}, bf16[320,320]{1,0:T(8,128)(2,1)}, u32[]{:S(2)}) copy-start(bf16[320,320]{1,0:T(8,128)(2,1)} %constant.34.clone.low_ref) | copy-start | bytes 614404
  0.6 33.7 %copy-start.3 = (bf16[320,320]{1,0:T(8,128)(2,1)S(1)}, bf16[320,320]{1,0:T(8,128)(2,1)}, u32[]{:S(2)}) copy-start(bf16[320,320]{1,0:T(8,128)(2,1)} %constant.33.clone.high_ref) | copy-start | bytes 614404
  1.4 71.1 %copy-start.4 = (bf16[4,256,320]{2,1,0:T(8,128)(2,1)S(1)}, bf16[4,256,320]{2,1,0:T(8,128)(2,1)}, u32[]{:S(2)}) copy-start(bf16[4,256,320]{2,1,0:T(8,128)(2,1)} %constant.38.clone.yl_ref) | copy-start | bytes 1966084
  1.4 71.1 %copy-start.5 = (bf16[4,256,320]{2,1,0:T(8,128)(2,1)S(1)}, bf16[4,256,320]{2,1,0:T(8,128)(2,1)}, u32[]{:S(2)}) copy-start(bf16[4,256,320]{2,1,0:T(8,128)(2,1)} %constant.37.clone.yh_ref) | copy-start | bytes 1966084
  1.4 71.1 %copy-start.6 = (bf16[2,256,256]{2,1,0:T(8,128)(2,1)S(1)}, bf16[2,256,256]{2,1,0:T(8,128)(2,1)}, u32[]{:S(2)}) copy-start(bf16[2,256,256]{2,1,0:T(8,128)(2,1)} %constant.36.clone.zl_ref) | copy-start | bytes 786436
  1.4 71.1 %copy-start.7 = (bf16[2,256,256]{2,1,0:T(8,128)(2,1)S(1)}, bf16[2,256,256]{2,1,0:T(8,128)(2,1)}, u32[]{:S(2)}) copy-start(bf16[2,256,256]{2,1,0:T(8,128)(2,1)} %constant.35.clone.zh_ref) | copy-start | bytes 786436
  34.3 49.2 %copy-start.1 = (f32[7,24,324]{2,1,0:T(8,128)S(1)}, f32[7,24,324]{2,1,0:T(8,128)}, u32[]{:S(2)}) copy-start(f32[7,24,324]{2,1,0:T(8,128)} %block_residual_ref.1) | copy-start | bytes 653188
  34.3 49.2 %copy-start.8 = (f32[7,24,324]{2,1,0:T(8,128)S(1)}, f32[7,24,324]{2,1,0:T(8,128)}, u32[]{:S(2)}) copy-start(f32[7,24,324]{2,1,0:T(8,128)} %block_ref.3) | copy-start | bytes 653188
  34.3 49.2 %copy-start.9 = (s32[24]{0:T(128)S(1)}, s32[24]{0:T(128)}, u32[]{:S(2)}) copy-start(s32[24]{0:T(128)} %species_ref.1) | copy-start | bytes 292
  76.9 37.5 %all-to-all-start.2 = ((f32[256,8,128]{2,1,0:T(8,128)}), f32[256,8,128]{2,1,0:T(8,128)S(1)}, u32[]{:S(2)}, u32[]{:S(2)}) async-start(f32[256,8,128]{2,1,0:T(8,128)} %bitcast.7), calls=%async_computation.2 | async-start | bytes 2097152 | tf_op jit(solution)/shard_map/all_to_all | solution.py:447
  83.6 3.0 %copy-start = (f32[7,8,80,320]{3,2,1,0:T(8,128)S(1)}, f32[7,8,80,320]{3,2,1,0:T(8,128)}, u32[]{:S(2)}) copy-start(f32[7,8,80,320]{3,2,1,0:T(8,128)} %density_ref.1) | copy-start | bytes 17203204
